TPU v7x, 256 devices: a whole 4x4x8 slice. The times are simulated.
256 devices in a mesh: head: 4 (over z_hi), outer: 4 (over z_lo, core), inner: 16 (over y, x).
Axes of the slice: x: 4, y: 4, z: 8 (z_hi: 4, z_lo: 2; z = z_hi * 2 + z_lo), core: 2. Of those that a mesh axis runs over, the one named last changes fastest.
Arguments:
- query_nope: bfloat16 [8192, 2048], P(('outer', 'inner'), 'head'), may hold values from -6 to 6
- query_rope: bfloat16 [8192, 1024], P(('outer', 'inner'), 'head'), may hold values from -8 to 8
- cache: bfloat16 [8192, 576], P(('outer', 'inner')), may hold values from -8 to 8
- span_ids: int32 [128], P(('outer', 'inner')), may hold values from 0 to 127, as said below
- key_up: bfloat16 [512, 2048], P(None, 'head'), may hold values from -0.25 to 0.25
- value_up: bfloat16 [512, 2048], P(None, 'head'), may hold values from -1.5 to 1.5
- out_proj: bfloat16 [2048, 2048], P('head'), may hold values from -1.1953125 to 1.1953125
Outputs:
- mixed: bfloat16 [8192, 2048], P(('outer', 'inner'), 'head')
Inputs may be any that keep to these rules, and one draw needn't show every extreme that they name: `span_ids`: each of 0 to 127 appears once; entries 2 r and 2 r + 1 belong to storage rows r * 128 to (r + 1) * 128 - 1.
All inputs are finite; a program needn't handle non-finite values.
Results may differ from a plain program's by a relative error of at most 0.014.
Values may be sent and summed in bfloat16 or wider, within the bound.
A program may use at most 64 MiB of HBM per device.

v0:
```python
import math

import jax
import jax.numpy as jnp
from jax import lax
from jax.sharding import Mesh
from jax.sharding import PartitionSpec as P

LATENT = 512
ROPE = 64
NOPE = 128
VDIM = 128
SPAN = 64
OUTER_INNER = ("outer_0", "outer_1", "inner_0", "inner_1")


lowest_start = -1e30


def joined_along(parts, dim):
    lengths = list(parts.shape[1:])
    lengths[dim] *= parts.shape[0]
    return jnp.moveaxis(parts, 0, dim).reshape(lengths)


def from_everyone(array, axis):
    count = lax.axis_size(axis)
    return lax.all_to_all(
        jnp.broadcast_to(array[None], (count, *array.shape)), axis, 0, 0, tiled=True
    )


def collect(array, axis, dim):
    return joined_along(from_everyone(array, axis), dim)


def all_blocks(array, axes, sequence):
    parts = array
    for k in sequence:
        parts = lax.all_gather(parts, axes[k])
    done = sequence[::-1]
    back = [done.index(k) for k in range(len(axes))]
    parts = parts.transpose(*back, *range(len(axes), parts.ndim))
    return parts.reshape(-1, *array.shape)


def gather_axes(array, axes, sequence, dim):
    return joined_along(all_blocks(array, axes, sequence), dim)


def split_up(array, dim, count):
    before, after = (array.shape[:dim], array.shape[dim + 1 :])
    return jnp.moveaxis(array.reshape(*before, count, -1, *after), dim, 0)


def sent_and_summed(array, axis, dim):
    count = lax.axis_size(axis)
    parts = lax.all_to_all(split_up(array, dim, count), axis, 0, 0, tiled=True)
    return jnp.sum(parts.astype(jnp.float32), axis=0)


def shards(query_nope, query_rope, cache, span_ids, key_up, value_up, out_proj):
    rows_dev = cache.shape[0]
    heads_dev = key_up.shape[1] // NOPE
    softmax_scale = (NOPE + ROPE) ** (-0.5)
    owners = collect(span_ids, OUTER_INNER, 0)
    span_count = owners.shape[0]
    offsets = jnp.arange(SPAN, dtype=jnp.int32)
    query_pos = (span_ids[:, None] * SPAN + offsets[None, :]).reshape(rows_dev)
    row_pos = jnp.tile(query_pos, heads_dev)
    query_heads = query_nope.reshape(rows_dev, heads_dev, NOPE)
    key_weight = key_up.reshape(LATENT, heads_dev, NOPE)
    q_latent = jnp.einsum(
        "shd,chd->hsc", query_heads, key_weight, preferred_element_type=jnp.float32
    ).astype(jnp.bfloat16)
    q_rotary = jnp.transpose(query_rope.reshape(rows_dev, heads_dev, ROPE), (1, 0, 2))
    queries = jnp.concatenate([q_latent, q_rotary], axis=2).reshape(
        heads_dev * rows_dev, LATENT + ROPE
    )
    span_slots = jnp.arange(span_count, dtype=jnp.int32)
    total_rows = heads_dev * rows_dev
    start_state = (
        jnp.full((total_rows,), lowest_start, jnp.float32),
        jnp.zeros((total_rows,), jnp.float32),
        jnp.zeros((total_rows, LATENT), jnp.float32),
    )
    segment = gather_axes(cache, OUTER_INNER, (0, 2, 3, 1), 0)
    length = segment.shape[0]
    seg_rows = jnp.arange(length, dtype=jnp.int32)
    seg_spans = seg_rows // SPAN
    span_now = jnp.sum(
        jnp.where(seg_spans[:, None] == span_slots[None, :], owners[None, :], 0), axis=1
    )
    key_pos = span_now * SPAN + seg_rows % SPAN
    block_rows = math.gcd(length, 2048)

    def one_block(step_index, status):
        running_max, running_sum, numerator = status
        key_block = lax.dynamic_slice_in_dim(segment, step_index * block_rows, block_rows, 0)
        block_pos = lax.dynamic_slice_in_dim(key_pos, step_index * block_rows, block_rows, 0)
        scores = (
            lax.dot_general(
                queries, key_block, (((1,), (1,)), ((), ())), preferred_element_type=jnp.float32
            )
            * softmax_scale
        )
        visible = block_pos[None, :] <= row_pos[:, None]
        scores = jnp.where(visible, scores, -jnp.inf)
        new_max = jnp.maximum(running_max, jnp.max(scores, axis=1))
        rescale = jnp.exp(running_max - new_max)
        weights = jnp.exp(scores - new_max[:, None])
        running_sum = running_sum * rescale + jnp.sum(weights, axis=1)
        numerator = numerator * rescale[:, None] + jnp.dot(
            weights.astype(jnp.bfloat16), key_block[:, :LATENT], preferred_element_type=jnp.float32
        )
        return (new_max, running_sum, numerator)

    result_state = lax.fori_loop(0, length // block_rows, one_block, start_state)
    running_sum = result_state[1]
    numerator = result_state[2]
    latent_out = (
        (numerator / running_sum[:, None]).astype(jnp.bfloat16).reshape(heads_dev, rows_dev, LATENT)
    )
    value_weight = value_up.reshape(LATENT, heads_dev, VDIM)
    head_out = jnp.einsum(
        "hsc,chd->shd", latent_out, value_weight, preferred_element_type=jnp.float32
    ).astype(jnp.bfloat16)
    head_out = head_out.reshape(rows_dev, heads_dev * VDIM)
    head_part = jnp.dot(head_out, out_proj, preferred_element_type=jnp.float32)
    return sent_and_summed(head_part.astype(jnp.bfloat16), "head", 1).astype(jnp.bfloat16)


def solution(mesh):
    finer = Mesh(
        mesh.devices.reshape(mesh.shape["head"], 2, 2, 4, 4),
        ("head", "outer_0", "outer_1", "inner_0", "inner_1"),
    )
    return jax.shard_map(
        shards,
        mesh=finer,
        in_specs=(
            P(OUTER_INNER, "head"),
            P(OUTER_INNER, "head"),
            P(OUTER_INNER, None),
            P(OUTER_INNER),
            P(None, "head"),
            P(None, "head"),
            P("head", None),
        ),
        out_specs=P(OUTER_INNER, "head"),
        check_vma=False,
    )
```

profile of v0, /device:TPU:32, one launch (start us, length us, event | category | flops | bytes accessed | tf_op | source)
XLA Modules:
  0.0 224.6 jit_solution(1577337936324060790)
XLA Ops:
  6.5 0.0 copy-start
  6.5 0.0 copy-start.5
  6.5 0.0 copy-start.4
  6.5 0.0 copy-start.2
  6.5 0.0 copy-start.3
  6.5 0.0 all-gather.8.cloned.1.call-start
  6.6 6.6 %all-gather = bf16[256,576]{0,1:T(8,128)(2,1)S(1)} all-gather(bf16[128,576]{0,1:T(8,128)(2,1)} %param.11), channel_id=2, replica_groups=mesh['head'=4,'outer_0'=2,'outer_1'=2,'inner_0'=4,'inner_1'=4] {'outer_0'}, dimensions={0}, use_global_device_ids=true | all-gather | bytes 442368 | tf_op jit(solution)/shard_map/all_gather | solution.py:40
  13.2 0.7 copy_bitcast_fusion
  14.0 0.0 all-gather.8.cloned.1.call-update
  14.0 0.0 all-gather.10.cloned.1.call-start
  14.0 29.7 %all-gather.8.cloned.1.call-done = bf16[8,128,576]{1,2,0:T(8,128)(2,1)} async-done(((bf16[2,128,576]{1,2,0:T(8,128)(2,1)}), bf16[8,128,576]{1,2,0:T(8,128)(2,1)}) %all-gather.8.cloned.1.call-update) | async-done | bytes 1179664 | tf_op jit(solution)/shard_map/all_gather | solution.py:40
  43.7 0.0 all-gather.10.cloned.1.call-update
  43.7 0.0 all-gather.12.cloned.1.call-start
  43.8 57.4 %all-gather.10.cloned.1.call-done = bf16[16,2,128,576]{2,3,1,0:T(8,128)(2,1)} async-done(((bf16[4,2,128,576]{2,3,1,0:T(8,128)(2,1)}), bf16[16,2,128,576]{2,3,1,0:T(8,128)(2,1)}) %all-gather.10.cloned.1.call-update) | async-done | bytes 4718608 | tf_op jit(solution)/shard_map/all_gather | solution.py:40
  101.2 0.0 all-gather.12.cloned.1.call-update
  101.2 0.0 copy-done.5
  101.2 0.6 broadcast_in_dim.54
  101.9 8.0 %all-to-all-start = ((s32[64,1,2]{2,1,0:T(1,128)}), s32[64,1,2]{2,1,0:T(1,128)S(1)}, u32[]{:S(2)}, u32[]{:S(2)}) async-start(s32[64,1,2]{2,1,0:T(1,128)} %broadcast_in_dim.54), calls=%async_computation | async-start | bytes 65536 | tf_op jit(solution)/shard_map/all_to_all | solution.py:28
  109.9 0.0 copy-done.4
  109.9 0.1 copy.46
  110.0 0.1 copy.47
  110.1 0.0 copy-done.2
  110.1 0.0 copy-done.3
  110.2 0.3 convolution_convert_fusion.1
  110.5 0.9 pad_maximum_fusion
  111.4 0.1 iota_add_fusion
  111.5 0.1 add.77
  111.5 2.0 copy.52
  113.6 3.3 %all-to-all-done = s32[64,1,2]{2,1,0:T(1,128)S(1)} async-done(((s32[64,1,2]{2,1,0:T(1,128)}), s32[64,1,2]{2,1,0:T(1,128)S(1)}, u32[]{:S(2)}, u32[]{:S(2)}) %all-to-all-start) | async-done | bytes 544 | tf_op jit(solution)/shard_map/all_to_all | solution.py:28
  116.9 0.5 broadcast.86
  117.4 0.7 reduce.4
  118.1 0.1 broadcast_in_dim.55
  118.2 2.5 %select_reduce_fusion = s32[8192]{0:T(1024)S(1)} fusion(s32[128]{0:T(128)S(1)} %broadcast_in_dim.55, s32[8192]{0:T(1024)S(1)} %add_select_fusion), kind=kLoop, calls=%fused_computation.18 | loop fusion | flops 3137536 | bytes 66048 | tf_op jit(solution)/shard_map/reduce_sum | solution.py:91
  120.8 9.7 %all-gather.12.cloned.1.call-done = bf16[8,4,2,128,576]{3,4,2,1,0:T(8,128)(2,1)} async-done(((bf16[4,4,2,128,576]{3,4,2,1,0:T(8,128)(2,1)}), bf16[8,4,2,128,576]{3,4,2,1,0:T(8,128)(2,1)}) %all-gather.12.cloned.1.call-update) | async-done | bytes 9437200 | tf_op jit(solution)/shard_map/all_gather | solution.py:40
  130.5 14.1 %copy.51 = bf16[2,2,4,4,128,576]{5,4,3,2,1,0:T(8,128)(2,1)} copy(bf16[2,2,4,4,128,576]{4,5,0,2,3,1:T(8,128)(2,1)} %bitcast.54) | data formatting | bytes 18874368
  144.6 49.4 %while.18 = (s32[]{:T(128)}, f32[512]{0:T(512)S(1)}, f32[512]{0:T(512)S(1)}, f32[512,512]{1,0:T(8,128)S(1)}, s32[8192]{0:T(1024)S(1)}, /*index=5*/bf16[8192,576]...) while((s32[]{:T(128)}, f32[512]{0:T(512)S(1)}, ...), condition=%wide.region_4.5_spmd.clone, body=%wide.region_1.4_spmd.clone.sunk | while | flops 2290878976 | bytes 36893396 | solution.py:118
  144.6 5.9 %fusion.48 = (f32[512]{0:T(512)S(1)}, f32[512,2048]{0,1:T(8,128)}) fusion(bf16[512,576]{1,0:T(8,128)(2,1)} %get-tuple-element.316, bf16[8192,576]{1,0:T(8,128)(2,1)} %get-tuple-element.315, s32[]{:T(128)S(6)} %select_n.48, s32[512]{0:T(512)S(1)} %broadcast_bitcast_fusion.2, s32[2048]{0:T(1024)S(1)} %dynamic_slice.23), kind=kOutput, calls=%fused_computation.45.clone.1 | convolution fusion | flops 1212153344 | bytes 7483396 | tf_op jit(solution)/shard_map/while/body/eval_jaxpr/dot_general | solution.py:102
  150.6 0.0 copy-start.1
  150.6 3.0 %fusion.49 = f32[512]{0:T(512)S(1)} fusion(f32[512,2048]{0,1:T(8,128)} %get-tuple-element.283, f32[512]{0:T(512)S(1)} %select_maximum_fusion.2), kind=kLoop, calls=%fused_computation.4.clone.1 | loop fusion | flops 2096640 | bytes 4198400 | tf_op jit(solution)/shard_map/while/body/eval_jaxpr/reduce_sum | solution.py:112
  153.5 0.5 copy-done.1
  154.0 2.9 %fusion.51 = f32[512,512]{1,0:T(8,128)S(1)} fusion(bf16[8192,576]{1,0:T(8,128)(2,1)} %get-tuple-element.315, s32[]{:T(128)S(6)} %select_n.48, f32[512,2048]{0,1:T(8,128)S(1)} %copy-done.1, f32[512]{0:T(512)S(1)} %select_maximum_fusion.2, f32[512,512]{1,0:T(8,128)S(1)} %get-tuple-element.301, f32[512]{0:T(512)S(1)} %get-tuple-element.285, pred[]{:T(512)S(6)} %compare.8), kind=kOutput, calls=%fused_computation.9.clone.1 | convolution fusion | flops 1076625408 | bytes 8392709 | tf_op jit(solution)/shard_map/while/body/eval_jaxpr/dot_general | solution.py:113
  157.0 5.9 %fusion.48 = (f32[512]{0:T(512)S(1)}, f32[512,2048]{0,1:T(8,128)}) fusion(bf16[512,576]{1,0:T(8,128)(2,1)} %get-tuple-element.316, bf16[8192,576]{1,0:T(8,128)(2,1)} %get-tuple-element.315, s32[]{:T(128)S(6)} %select_n.48, s32[512]{0:T(512)S(1)} %broadcast_bitcast_fusion.2, s32[2048]{0:T(1024)S(1)} %dynamic_slice.23), kind=kOutput, calls=%fused_computation.45.clone.1 | convolution fusion | flops 1212153344 | bytes 7483396 | tf_op jit(solution)/shard_map/while/body/eval_jaxpr/dot_general | solution.py:102
  162.9 0.0 copy-start.1
  162.9 3.0 %fusion.49 = f32[512]{0:T(512)S(1)} fusion(f32[512,2048]{0,1:T(8,128)} %get-tuple-element.283, f32[512]{0:T(512)S(1)} %select_maximum_fusion.2), kind=kLoop, calls=%fused_computation.4.clone.1 | loop fusion | flops 2096640 | bytes 4198400 | tf_op jit(solution)/shard_map/while/body/eval_jaxpr/reduce_sum | solution.py:112
  165.9 0.5 copy-done.1
  166.4 2.9 %fusion.51 = f32[512,512]{1,0:T(8,128)S(1)} fusion(bf16[8192,576]{1,0:T(8,128)(2,1)} %get-tuple-element.315, s32[]{:T(128)S(6)} %select_n.48, f32[512,2048]{0,1:T(8,128)S(1)} %copy-done.1, f32[512]{0:T(512)S(1)} %select_maximum_fusion.2, f32[512,512]{1,0:T(8,128)S(1)} %get-tuple-element.301, f32[512]{0:T(512)S(1)} %get-tuple-element.285, pred[]{:T(512)S(6)} %compare.8), kind=kOutput, calls=%fused_computation.9.clone.1 | convolution fusion | flops 1076625408 | bytes 8392709 | tf_op jit(solution)/shard_map/while/body/eval_jaxpr/dot_general | solution.py:113
  169.3 5.9 %fusion.48 = (f32[512]{0:T(512)S(1)}, f32[512,2048]{0,1:T(8,128)}) fusion(bf16[512,576]{1,0:T(8,128)(2,1)} %get-tuple-element.316, bf16[8192,576]{1,0:T(8,128)(2,1)} %get-tuple-element.315, s32[]{:T(128)S(6)} %select_n.48, s32[512]{0:T(512)S(1)} %broadcast_bitcast_fusion.2, s32[2048]{0:T(1024)S(1)} %dynamic_slice.23), kind=kOutput, calls=%fused_computation.45.clone.1 | convolution fusion | flops 1212153344 | bytes 7483396 | tf_op jit(solution)/shard_map/while/body/eval_jaxpr/dot_general | solution.py:102
  175.3 0.0 copy-start.1
  175.3 3.0 %fusion.49 = f32[512]{0:T(512)S(1)} fusion(f32[512,2048]{0,1:T(8,128)} %get-tuple-element.283, f32[512]{0:T(512)S(1)} %select_maximum_fusion.2), kind=kLoop, calls=%fused_computation.4.clone.1 | loop fusion | flops 2096640 | bytes 4198400 | tf_op jit(solution)/shard_map/while/body/eval_jaxpr/reduce_sum | solution.py:112
  178.3 0.5 copy-done.1
  178.7 2.9 %fusion.51 = f32[512,512]{1,0:T(8,128)S(1)} fusion(bf16[8192,576]{1,0:T(8,128)(2,1)} %get-tuple-element.315, s32[]{:T(128)S(6)} %select_n.48, f32[512,2048]{0,1:T(8,128)S(1)} %copy-done.1, f32[512]{0:T(512)S(1)} %select_maximum_fusion.2, f32[512,512]{1,0:T(8,128)S(1)} %get-tuple-element.301, f32[512]{0:T(512)S(1)} %get-tuple-element.285, pred[]{:T(512)S(6)} %compare.8), kind=kOutput, calls=%fused_computation.9.clone.1 | convolution fusion | flops 1076625408 | bytes 8392709 | tf_op jit(solution)/shard_map/while/body/eval_jaxpr/dot_general | solution.py:113
  181.7 5.9 %fusion.48 = (f32[512]{0:T(512)S(1)}, f32[512,2048]{0,1:T(8,128)}) fusion(bf16[512,576]{1,0:T(8,128)(2,1)} %get-tuple-element.316, bf16[8192,576]{1,0:T(8,128)(2,1)} %get-tuple-element.315, s32[]{:T(128)S(6)} %select_n.48, s32[512]{0:T(512)S(1)} %broadcast_bitcast_fusion.2, s32[2048]{0:T(1024)S(1)} %dynamic_slice.23), kind=kOutput, calls=%fused_computation.45.clone.1 | convolution fusion | flops 1212153344 | bytes 7483396 | tf_op jit(solution)/shard_map/while/body/eval_jaxpr/dot_general | solution.py:102
  187.6 0.0 copy-start.1
  187.6 3.0 %fusion.49 = f32[512]{0:T(512)S(1)} fusion(f32[512,2048]{0,1:T(8,128)} %get-tuple-element.283, f32[512]{0:T(512)S(1)} %select_maximum_fusion.2), kind=kLoop, calls=%fused_computation.4.clone.1 | loop fusion | flops 2096640 | bytes 4198400 | tf_op jit(solution)/shard_map/while/body/eval_jaxpr/reduce_sum | solution.py:112
  190.6 0.5 copy-done.1
  191.1 2.9 %fusion.51 = f32[512,512]{1,0:T(8,128)S(1)} fusion(bf16[8192,576]{1,0:T(8,128)(2,1)} %get-tuple-element.315, s32[]{:T(128)S(6)} %select_n.48, f32[512,2048]{0,1:T(8,128)S(1)} %copy-done.1, f32[512]{0:T(512)S(1)} %select_maximum_fusion.2, f32[512,512]{1,0:T(8,128)S(1)} %get-tuple-element.301, f32[512]{0:T(512)S(1)} %get-tuple-element.285, pred[]{:T(512)S(6)} %compare.8), kind=kOutput, calls=%fused_computation.9.clone.1 | convolution fusion | flops 1076625408 | bytes 8392709 | tf_op jit(solution)/shard_map/while/body/eval_jaxpr/dot_general | solution.py:113
  194.0 0.1 divide_convert_fusion
  194.2 1.3 convolution_convert_fusion.2
  195.5 0.0 copy-done
  195.5 0.5 convolution_convert_fusion
  196.0 21.3 %all_to_all.11 = bf16[4,128,512]{2,1,0:T(8,128)(2,1)S(1)} all-to-all(bf16[4,128,512]{2,1,0:T(8,128)(2,1)S(1)} %bitcast.58), channel_id=1, replica_groups=mesh['head'=4,'outer_0'=2,'outer_1'=2,'inner_0'=4,'inner_1'=4] {'head'}, dimensions={0} | all-to-all | bytes 1048576 | tf_op jit(solution)/shard_map/all_to_all | solution.py:58
  217.3 0.7 reduce_sum.35
  (27 shorter events, 0.2 us)
Async XLA Ops:
  6.5 189.0 %copy-start = (bf16[512,2048]{1,0:T(8,128)(2,1)S(1)}, bf16[512,2048]{1,0:T(8,128)(2,1)}, u32[]{:S(2)}) copy-start(bf16[512,2048]{1,0:T(8,128)(2,1)} %param.15) | copy-start | bytes 6291460
  6.5 94.7 %copy-start.5 = (s32[2]{0:T(128)S(1)}, s32[2]{0:T(128)}, u32[]{:S(2)}) copy-start(s32[2]{0:T(128)} %param.12) | copy-start | bytes 28
  6.5 103.3 %copy-start.4 = (bf16[128,256]{1,0:T(8,128)(2,1)S(1)}, bf16[128,256]{1,0:T(8,128)(2,1)}, u32[]{:S(2)}) copy-start(bf16[128,256]{1,0:T(8,128)(2,1)} %param.10) | copy-start | bytes 196612
  6.5 103.6 %copy-start.2 = (bf16[512,512]{1,0:T(8,128)(2,1)S(1)}, bf16[512,512]{1,0:T(8,128)(2,1)}, u32[]{:S(2)}) copy-start(bf16[512,512]{1,0:T(8,128)(2,1)} %param.13) | copy-start | bytes 1572868
  6.5 103.6 %copy-start.3 = (bf16[128,512]{1,0:T(8,128)(2,1)S(1)}, bf16[128,512]{1,0:T(8,128)(2,1)}, u32[]{:S(2)}) copy-start(bf16[128,512]{1,0:T(8,128)(2,1)} %param.9) | copy-start | bytes 393220
  6.5 37.1 %all-gather.8.cloned.1.call-start = ((), (), s32[]{:S(2)}) async-start(), calls=%async_computation.2 | async-start | bytes 1474560 | tf_op jit(solution)/shard_map/all_gather | solution.py:40
  14.0 87.2 %all-gather.10.cloned.1.call-start = ((), (), s32[]{:S(2)}) async-start(), calls=%async_computation.3 | async-start | bytes 5898240 | tf_op jit(solution)/shard_map/all_gather | solution.py:40
  43.7 86.8 %all-gather.12.cloned.1.call-start = ((), (), s32[]{:S(2)}) async-start(), calls=%async_computation.4 | async-start | bytes 14155776 | tf_op jit(solution)/shard_map/all_gather | solution.py:40
  101.9 15.0 %all-to-all-start = ((s32[64,1,2]{2,1,0:T(1,128)}), s32[64,1,2]{2,1,0:T(1,128)S(1)}, u32[]{:S(2)}, u32[]{:S(2)}) async-start(s32[64,1,2]{2,1,0:T(1,128)} %broadcast_in_dim.54), calls=%async_computation | async-start | bytes 65536 | tf_op jit(solution)/shard_map/all_to_all | solution.py:28
  150.6 3.4 %copy-start.1 = (f32[512,2048]{0,1:T(8,128)S(1)}, f32[512,2048]{0,1:T(8,128)}, u32[]{:S(2)}) copy-start(f32[512,2048]{0,1:T(8,128)} %get-tuple-element.283) | copy-start | bytes 12582916 | tf_op jit(solution)/shard_map/while
  162.9 3.4 %copy-start.1 = (f32[512,2048]{0,1:T(8,128)S(1)}, f32[512,2048]{0,1:T(8,128)}, u32[]{:S(2)}) copy-start(f32[512,2048]{0,1:T(8,128)} %get-tuple-element.283) | copy-start | bytes 12582916 | tf_op jit(solution)/shard_map/while
  175.3 3.4 %copy-start.1 = (f32[512,2048]{0,1:T(8,128)S(1)}, f32[512,2048]{0,1:T(8,128)}, u32[]{:S(2)}) copy-start(f32[512,2048]{0,1:T(8,128)} %get-tuple-element.283) | copy-start | bytes 12582916 | tf_op jit(solution)/shard_map/while
  187.6 3.4 %copy-start.1 = (f32[512,2048]{0,1:T(8,128)S(1)}, f32[512,2048]{0,1:T(8,128)}, u32[]{:S(2)}) copy-start(f32[512,2048]{0,1:T(8,128)} %get-tuple-element.283) | copy-start | bytes 12582916 | tf_op jit(solution)/shard_map/while
Sparse Core Ops, SparseCore 0:
  14.1 29.5 all-gather.7
  45.5 55.6 all-gather.9
  103.0 27.4 all-gather.11
where the time goes:
time: 228 us; the launch traced here: 225 us
  waiting for transfers between devices  100 us (44%)
  matrix products  37.5 us (16%)
  blocking collectives  27.9 us (12%)
  local copies, waits for them, and re-layouts  20.4 us (9%)
  other arithmetic  17.1 us (8%)
  between operations  13.3 us (6%)
  starting transfers between devices  8.1 us (4%)
    all_gather x3, waiting for transfers between devices, all_blocks(): parts = lax.all_gather(parts, axes[k])  96.8 us
    dot_general x4, matrix products, one_block(): lax.dot_general(queries, key_block, (((1,), (1,)), ((), ())), preferred_e...  23.7 us
    all_to_all x1, blocking collectives, sent_and_summed(): parts = lax.all_to_all(split_up(array, dim, count), axis, 0, 0, tiled=True)  21.3 us
    unnamed x12, local copies, waits for them, and re-layouts  14.3 us
    reduce_sum x4, other arithmetic, one_block(): running_sum = running_sum * rescale + jnp.sum(weights, axis=1)  11.9 us
    dot_general x4, matrix products, one_block(): jnp.dot(weights.astype(jnp.bfloat16), key_block[:, :LATENT], preferred_el...  11.6 us
    all_to_all x1, starting transfers between devices, from_everyone(): lax.all_to_all(jnp.broadcast_to(array[None], (count, *array.shape)), axis...  7.98 us
    all_gather x1, blocking collectives, all_blocks(): parts = lax.all_gather(parts, axes[k])  6.63 us
  transfers between devices with their start and end apart: 4, of which 4 were waited for; matrix products, arithmetic and copies ran while one was open for 4% of the time, Pallas kernels for 0%

commit v1 on v0

v1 whole, which is shorter than its diff:
```python
import jax
import jax.numpy as jnp
from jax import lax
from jax.experimental import pallas as pl
from jax.experimental.pallas import tpu as pltpu
from jax.sharding import PartitionSpec as P

LATENT = 512
ROPE = 64
NOPE = 128
SPAN = 64
HEADS_DEV = 4
ROWS = 128
WIDTH = LATENT + ROPE
QWIDTH = HEADS_DEV * (NOPE + ROPE)
R = 4
SUB = ROWS // R
UNIT = HEADS_DEV * 4 * SUB
KROWS = ROWS + 16
HALVES = ((0, 64), (64, 80))
SCALE = (NOPE + ROPE) ** -0.5 * 1.4426950408889634
LOG2E = 1.4426950408889634
LOWEST = -1e30
MESH = pl.DeviceIdType.MESH
TN = (((1,), (1,)), ((), ()))
NN = (((1,), (0,)), ((), ()))
f32 = jnp.float32
bf16 = jnp.bfloat16
CHUNKS = ((0, 4, 8, 12), (1, 3, 5, 7), (2, 6, 9, 11), (10, 13, 14, 15))


def kernel(
    span_ref, qn_ref, qr_ref, k_ref, ku_ref, vu_ref, op_ref, out_ref,
    kbuf, qx, qpos, ku, vu, op, qs, qc, s_sc, m_sc, pbuf, stat, rbuf, rstat,
    ybuf, y1, ysum, y2,
    load_sem, kr_sem, ks_sem, qr_sem, qs_sem, pr_sem, ps_sem, rr_sem, rs_sem, tr_sem, ts_sem,
    zr_sem, zs_sem,
):
    h = lax.axis_index("head")
    o = lax.axis_index("outer")
    i = lax.axis_index("inner")
    zl, c = o // 2, o % 2
    y, x = i // 4, i % 4
    z = h * 2 + zl

    def at_z(zz):
        return (zz // 2, (zz % 2) * 2 + c, i)

    sib = (h, zl * 2 + 1 - c, i)
    yp = (h, o, ((y + 1) % 4) * 4 + x)
    ym = (h, o, ((y + 3) % 4) * 4 + x)
    zp = at_z((z + 1) % 8)
    zm = at_z((z + 7) % 8)
    xs = [None] + [(h, o, y * 4 + (x + d) % 4) for d in (1, 2, 3)]
    hp = ((h + 1) % 4, o, i)
    hm = ((h + 3) % 4, o, i)

    loads = [
        pltpu.make_async_copy(k_ref, kbuf.at[0, pl.ds(0, ROWS)], load_sem.at[0]),
        pltpu.make_async_copy(qn_ref, qx.at[0, :, pl.ds(0, 512)], load_sem.at[1]),
        pltpu.make_async_copy(qr_ref, qx.at[0, :, pl.ds(512, 256)], load_sem.at[2]),
        pltpu.make_async_copy(ku_ref, ku, load_sem.at[3]),
        pltpu.make_async_copy(vu_ref, vu, load_sem.at[4]),
        pltpu.make_async_copy(op_ref, op, load_sem.at[5]),
    ]
    for copy in loads:
        copy.start()
    barrier = pltpu.get_barrier_semaphore()
    for partner in (sib, yp, ym, zp, zm, xs[1], xs[2], xs[3], hp, hm):
        pl.semaphore_signal(barrier, inc=1, device_id=partner, device_id_type=MESH)
    first = span_ref[0].astype(f32)
    second = span_ref[1].astype(f32)
    lane = lax.broadcasted_iota(jnp.int32, (16, 128), 1)
    row = lax.broadcasted_iota(jnp.int32, (16, 128), 0)
    kbuf[0, ROWS:KROWS, :] = jnp.zeros((16, WIDTH), bf16)
    kbuf[0, ROWS:KROWS, 0:128] = jnp.where(lane < SPAN, first, second).astype(bf16)
    qpos[0] = jnp.where(row < 8, first, second).astype(bf16)
    pl.semaphore_wait(barrier, 10)

    sends = []

    def send(src, dst, s_sem, r_sem, device):
        copy = pltpu.make_async_remote_copy(
            src_ref=src, dst_ref=dst, send_sem=s_sem, recv_sem=r_sem,
            device_id=device, device_id_type=MESH,
        )
        copy.start()
        sends.append(copy)

    count = [0]

    def half(slot, b):
        begin, size = HALVES[b]
        return kbuf.at[slot, pl.ds(begin, size)]

    def send_k(slot, b, there, device):
        send(half(slot, b), half(there, b), ks_sem.at[count[0]], kr_sem.at[there, b], device)
        count[0] += 1

    def wait_k(slot, b):
        pltpu.make_async_copy(half(slot, b), half(slot, b), kr_sem.at[slot, b]).wait()

    def qpart(slot, r):
        return qx.at[slot, pl.ds(r * SUB, SUB)]

    def send_q(slot, r, there, device, s_sem):
        send(qpart(slot, r), qpart(there, r), s_sem, qr_sem.at[there, r], device)

    def wait_q(slot, r):
        pltpu.make_async_copy(qpart(slot, r), qpart(slot, r), qr_sem.at[slot, r]).wait()

    loads[0].wait()
    send_k(0, 0, 3, yp)
    send_k(0, 1, 1, ym)
    send_k(0, 0, 8, zp)
    send_k(0, 1, 8, zm)
    send_k(0, 0, 4, sib)
    send_k(0, 1, 4, sib)
    send_k(0, 1, 3, yp)
    send_k(0, 0, 1, ym)
    loads[1].wait()
    loads[2].wait()
    for d in (1, 2, 3):
        send(qpos.at[0], qpos.at[4 - d], ps_sem.at[d - 1], pr_sem.at[4 - d], xs[d])
    for r in range(R):
        send_q(0, r, 3, xs[1], qs_sem.at[0, r])
        send_q(0, r, 1, xs[3], qs_sem.at[1, r])

    def build_q(r):
        rows = pl.ds(r * SUB, SUB)
        for head in range(HEADS_DEV):
            nope = qx[:, rows, head * NOPE : (head + 1) * NOPE].reshape(4 * SUB, NOPE)
            latent = lax.dot_general(
                nope, ku[:, head * NOPE : (head + 1) * NOPE], TN, preferred_element_type=f32
            )
            mine = pl.ds(head * 4 * SUB, 4 * SUB)
            qs[r, mine, 0:LATENT] = latent.astype(bf16)
            begin = HEADS_DEV * NOPE + head * ROPE
            qs[r, mine, LATENT:WIDTH] = qx[:, rows, begin : begin + ROPE].reshape(4 * SUB, ROPE)
        within = lax.broadcasted_iota(jnp.int32, (SUB, 128), 0).astype(f32)
        for d in range(4):
            span = qpos[d].astype(f32)[(r * SUB // SPAN) * 8 : (r * SUB // SPAN) * 8 + 1, :]
            pos = span * SPAN + (within + (r * SUB) % SPAN)
            for head in range(HEADS_DEV):
                qc[r, pl.ds(head * 4 * SUB + d * SUB, SUB), :] = pos
        m_sc[r] = jnp.full((UNIT, 128), LOWEST, f32)

    offset = lax.rem(lax.broadcasted_iota(jnp.int32, (1, 128), 1), SPAN).astype(f32)

    def scores(chunk, r):
        slots = CHUNKS[chunk]
        keys = jnp.concatenate([kbuf[s, 0:ROWS, :] for s in slots], axis=0)
        values = lax.dot_general(qs[r], keys, TN, preferred_element_type=f32)
        rowpos = qc[r]
        peak = m_sc[r]
        for j, s in enumerate(slots):
            keypos = kbuf[s, ROWS:KROWS, 0:128].astype(f32)[0:1, :] * SPAN + offset
            part = jnp.where(
                keypos <= rowpos, values[:, j * 128 : (j + 1) * 128] * SCALE, LOWEST
            )
            s_sc[r, :, s * 128 : (s + 1) * 128] = part
            peak = jnp.maximum(peak, part)
        m_sc[r] = peak

    def scores_for(chunk, low, high):
        def body(r, carry):
            scores(chunk, r)
            return carry

        lax.fori_loop(low, high, body, 0)

    def pass_z(slot):
        send_k(slot, 0, slot + 8, zp)
        send_k(slot, 1, slot + 8, zm)

    wait_k(8, 0)
    send_k(8, 0, 12, sib)
    wait_k(8, 1)
    send_k(8, 1, 12, sib)
    wait_k(3, 0)
    send_k(3, 0, 2, yp)
    send_k(3, 0, 11, zp)
    send_k(3, 0, 7, sib)
    wait_k(1, 1)
    send_k(1, 1, 2, ym)
    send_k(1, 1, 9, zm)
    send_k(1, 1, 5, sib)
    wait_q(3, 0)
    send_q(3, 0, 2, xs[1], qs_sem.at[2, 0])
    wait_k(3, 1)
    send_k(3, 1, 11, zm)
    send_k(3, 1, 7, sib)
    wait_k(1, 0)
    send_k(1, 0, 9, zp)
    send_k(1, 0, 5, sib)
    for d in (1, 2, 3):
        pltpu.make_async_copy(qpos.at[d], qpos.at[d], pr_sem.at[d]).wait()
    loads[3].wait()
    wait_q(1, 0)
    wait_q(2, 0)
    build_q(0)
    for slot in (4, 12):
        for b in (0, 1):
            wait_k(slot, b)
    scores(0, 0)
    wait_q(1, 1)
    send_q(1, 1, 2, xs[3], qs_sem.at[2, 1])
    wait_k(2, 0)
    send_k(2, 0, 10, zp)
    send_k(2, 0, 6, sib)
    wait_k(2, 1)
    send_k(2, 1, 10, zm)
    send_k(2, 1, 6, sib)
    wait_q(3, 1)
    wait_q(2, 1)
    build_q(1)
    scores_for(0, 1, 2)
    for slot in (5, 7):
        for b in (0, 1):
            wait_k(slot, b)
    wait_q(3, 2)
    send_q(3, 2, 2, xs[1], qs_sem.at[2, 2])
    scores_for(1, 0, 2)
    for slot in (11, 9):
        for b in (0, 1):
            wait_k(slot, b)
            send_k(slot, b, slot + 4, sib)
    for b in (0, 1):
        wait_k(6, b)
    wait_q(1, 2)
    wait_q(2, 2)
    build_q(2)
    scores_for(2, 0, 3)
    for b in (0, 1):
        wait_k(10, b)
        send_k(10, b, 14, sib)
    wait_q(1, 3)
    send_q(1, 3, 2, xs[3], qs_sem.at[2, 3])
    scores_for(0, 2, 3)
    scores_for(1, 2, 3)
    for slot in (13, 14, 15):
        for b in (0, 1):
            wait_k(slot, b)
    scores_for(3, 0, 3)
    wait_q(3, 3)
    wait_q(2, 3)
    build_q(3)
    for chunk in range(4):
        scores_for(chunk, 3, 4)
    loads[4].wait()

    def weigh(r):
        top = jnp.max(m_sc[r], axis=1, keepdims=True)
        wide = jnp.broadcast_to(top, (UNIT, 128))
        total = jnp.zeros((UNIT, 128), f32)
        acc = None
        for t in range(4):
            parts = []
            for j in range(4):
                begin = (t * 4 + j) * 128
                w = jnp.exp2(s_sc[r, :, begin : begin + 128] - wide)
                total = total + w
                parts.append(w.astype(bf16))
            latents = jnp.concatenate([kbuf[t * 4 + j, 0:ROWS, 0:LATENT] for j in range(4)], axis=0)
            piece = lax.dot_general(
                jnp.concatenate(parts, axis=1), latents, NN, preferred_element_type=f32
            )
            acc = piece if acc is None else acc + piece
        denom = jnp.sum(total, axis=1, keepdims=True)
        logs = top + jnp.log(denom) * LOG2E
        latent_out = (acc / denom).astype(bf16)
        for head in range(HEADS_DEV):
            mine = slice(head * 4 * SUB, (head + 1) * 4 * SUB)
            part = lax.dot_general(
                latent_out[mine], vu[:, head * 128 : (head + 1) * 128], NN,
                preferred_element_type=f32,
            ).astype(bf16)
            for d in range(4):
                pbuf[r, d, :, head * 128 : (head + 1) * 128] = part[d * SUB : (d + 1) * SUB]
            flat = jnp.transpose(jnp.broadcast_to(logs[mine], (128, 128)))
            stat[r, head : head + 1, :] = flat[0:1, :]
        for d in (1, 3, 2):
            send(pbuf.at[r, d], rbuf.at[r, d - 1], rs_sem.at[r, d - 1], rr_sem.at[r, d - 1], xs[d])
            send(stat.at[r], rstat.at[r, d - 1], ts_sem.at[r, d - 1], tr_sem.at[r, d - 1], xs[d])

    def merge(r):
        for d in (0, 1, 2):
            pltpu.make_async_copy(rbuf.at[r, d], rbuf.at[r, d], rr_sem.at[r, d]).wait()
            pltpu.make_async_copy(rstat.at[r, d], rstat.at[r, d], tr_sem.at[r, d]).wait()
        tiles = [stat[r]] + [rstat[r, d] for d in range(3)]
        columns = [
            jnp.transpose(tile)[d * SUB : (d + 1) * SUB, :] for d, tile in enumerate(tiles)
        ]
        heads = []
        for head in range(HEADS_DEV):
            logs = [col[:, head : head + 1] for col in columns]
            top = jnp.maximum(jnp.maximum(logs[0], logs[1]), jnp.maximum(logs[2], logs[3]))
            scale = [jnp.exp2(v - top) for v in logs]
            total = scale[0] + scale[1] + scale[2] + scale[3]
            where = slice(head * 128, (head + 1) * 128)
            acc = pbuf[r, 0, :, where].astype(f32) * scale[0]
            for d in range(3):
                acc = acc + rbuf[r, d, :, where].astype(f32) * scale[d + 1]
            heads.append((acc / total).astype(bf16))
        head_out = jnp.concatenate(heads, axis=1)
        for d in (2, 1, 3, 0):
            begin = pl.multiple_of(((h + d) % 4) * 512, 512)
            ybuf[r, d] = lax.dot_general(
                head_out, op[:, pl.ds(begin, 512)], NN, preferred_element_type=f32
            ).astype(bf16)
            if d == 2:
                send(
                    ybuf.at[r, 2, :, pl.ds(0, 256)], y1.at[r, 0],
                    zs_sem.at[r, 0], zr_sem.at[r, 0], hp,
                )
                send(
                    ybuf.at[r, 2, :, pl.ds(256, 256)], y1.at[r, 1],
                    zs_sem.at[r, 1], zr_sem.at[r, 1], hm,
                )

    def pass_on(r):
        for b in (0, 1):
            pltpu.make_async_copy(y1.at[r, b], y1.at[r, b], zr_sem.at[r, b]).wait()
        left = ybuf[r, 1, :, 0:256].astype(f32) + y1[r, 0].astype(f32)
        ysum[r, 0, :, 0:256] = left.astype(bf16)
        ysum[r, 0, :, 256:512] = ybuf[r, 1, :, 256:512]
        send(ysum.at[r, 0], y2.at[r, 0], zs_sem.at[r, 2], zr_sem.at[r, 2], hp)
        right = ybuf[r, 3, :, 256:512].astype(f32) + y1[r, 1].astype(f32)
        ysum[r, 1, :, 256:512] = right.astype(bf16)
        ysum[r, 1, :, 0:256] = ybuf[r, 3, :, 0:256]
        send(ysum.at[r, 1], y2.at[r, 1], zs_sem.at[r, 3], zr_sem.at[r, 3], hm)

    def finish(r):
        for b in (0, 1):
            pltpu.make_async_copy(y2.at[r, b], y2.at[r, b], zr_sem.at[r, 2 + b]).wait()
        total = ybuf[r, 0].astype(f32) + y2[r, 0].astype(f32) + y2[r, 1].astype(f32)
        out_ref[r * SUB : (r + 1) * SUB, :] = total.astype(bf16)

    weigh(0)
    weigh(1)
    weigh(2)
    loads[5].wait()
    merge(0)
    weigh(3)
    merge(1)
    pass_on(0)
    merge(2)
    pass_on(1)
    merge(3)
    pass_on(2)
    finish(0)
    pass_on(3)
    finish(1)
    finish(2)
    finish(3)
    for copy in sends:
        copy.wait_send()


def shards(query_nope, query_rope, cache, span_ids, key_up, value_up, out_proj):
    anywhere = pl.BlockSpec(memory_space=pl.ANY)
    dma = pltpu.SemaphoreType.DMA
    return pl.pallas_call(
        kernel,
        name="attend",
        out_shape=jax.ShapeDtypeStruct((ROWS, 512), bf16),
        in_specs=[pl.BlockSpec(memory_space=pltpu.SMEM)] + [anywhere] * 6,
        out_specs=pl.BlockSpec(memory_space=pltpu.VMEM),
        scratch_shapes=[
            pltpu.VMEM((16, KROWS, WIDTH), bf16),
            pltpu.VMEM((4, ROWS, QWIDTH), bf16),
            pltpu.VMEM((4, 16, 128), bf16),
            pltpu.VMEM((512, 512), bf16),
            pltpu.VMEM((512, 512), bf16),
            pltpu.VMEM((512, 2048), bf16),
            pltpu.VMEM((R, UNIT, WIDTH), bf16),
            pltpu.VMEM((R, UNIT, 128), f32),
            pltpu.VMEM((R, UNIT, 2048), f32),
            pltpu.VMEM((R, UNIT, 128), f32),
            pltpu.VMEM((R, 4, SUB, 512), bf16),
            pltpu.VMEM((R, 8, 128), f32),
            pltpu.VMEM((R, 3, SUB, 512), bf16),
            pltpu.VMEM((R, 3, 8, 128), f32),
            pltpu.VMEM((R, 4, SUB, 512), bf16),
            pltpu.VMEM((R, 2, SUB, 256), bf16),
            pltpu.VMEM((R, 2, SUB, 512), bf16),
            pltpu.VMEM((R, 2, SUB, 512), bf16),
            dma((6,)),
            dma((16, 2)),
            dma((40,)),
            dma((4, R)),
            dma((3, R)),
            dma((4,)),
            dma((3,)),
            dma((R, 3)),
            dma((R, 3)),
            dma((R, 3)),
            dma((R, 3)),
            dma((R, 4)),
            dma((R, 4)),
        ],
        compiler_params=pltpu.CompilerParams(
            collective_id=0, has_side_effects=True, vmem_limit_bytes=62 * 2**20
        ),
    )(span_ids, query_nope, query_rope, cache, key_up, value_up, out_proj)


def solution(mesh):
    rows = ("outer", "inner")
    return jax.shard_map(
        shards,
        mesh=mesh,
        in_specs=(
            P(rows, "head"),
            P(rows, "head"),
            P(rows, None),
            P(rows),
            P(None, "head"),
            P(None, "head"),
            P("head", None),
        ),
        out_specs=P(rows, "head"),
        check_vma=False,
    )
```

time: 228 us -> 62.2 us (0.27); the launches traced: 225 us -> 61.7 us
  waiting for transfers between devices: 100 us -> 0 us
  Pallas kernels: 0 us -> 58.5 us
  matrix products: 37.5 us -> 0 us
  blocking collectives: 27.9 us -> 0 us
  local copies, waits for them, and re-layouts: 20.4 us -> 3.27 us
  other arithmetic: 17.1 us -> 0 us
  between operations: 13.3 us -> 0.01 us
  starting transfers between devices: 8.1 us -> 0 us
    all_gather x3 -> x0, waiting for transfers between devices: 96.8 us -> none  [all_blocks(): parts = lax.all_gather(parts, axes[k])]
    pallas_call x0 -> x1, Pallas kernels: none -> 58.5 us  [shards(): pl.pallas_call(kernel, name='attend', out_shape=jax.ShapeDtypeStruct((ROW...]
    dot_general x11 -> x0, matrix products: 37.5 us -> none  [the longest x4 23.7 us: one_block(): lax.dot_general(queries, key_block, (((1,), (1,)), ((), ())), preferred_e...]
    all_to_all x1 -> x0, blocking collectives: 21.3 us -> none  [sent_and_summed(): parts = lax.all_to_all(split_up(array, dim, count), axis, 0, 0, tiled=True)]
    reduce_sum x6 -> x0, other arithmetic: 15.2 us -> none  [the longest x4 11.9 us: one_block(): running_sum = running_sum * rescale + jnp.sum(weights, axis=1)]
    unnamed x12 -> x2, local copies, waits for them, and re-layouts: 14.3 us -> 3.27 us
    all_to_all x1 -> x0, starting transfers between devices: 7.98 us -> none  [from_everyone(): lax.all_to_all(jnp.broadcast_to(array[None], (count, *array.shape)), axis...]
    all_gather x1 -> x0, blocking collectives: 6.63 us -> none  [all_blocks(): parts = lax.all_gather(parts, axes[k])]
  transfers between devices with their start and end apart: 4 -> 0, of which waited for: 4 -> 0; matrix products, arithmetic and copies ran while one was open for 4% -> 0% of each run, Pallas kernels for 0% -> 0%
where the time goes in v1:
time: 62.2 us; the launch traced here: 61.7 us
  Pallas kernels  58.5 us (94%)
  local copies, waits for them, and re-layouts  3.27 us (5%)
    pallas_call x1, Pallas kernels, shards(): pl.pallas_call(kernel, name='attend', out_shape=jax.ShapeDtypeStruct((ROW...  58.5 us
    unnamed x2, local copies, waits for them, and re-layouts  3.27 us

profile of v1, /device:TPU:32, one launch (start us, length us, event | category | flops | bytes accessed | tf_op | source)
XLA Modules:
  0.0 61.7 jit_solution(8012973358181259001)
XLA Ops:
  0.0 1.7 %copy.8.k_ref = bf16[128,576]{1,0:T(8,128)(2,1)} copy(bf16[128,576]{0,1:T(8,128)(2,1)} %param.9) | data formatting | bytes 294912 | tf_op args[2]
  1.7 58.5 %attend.1 = bf16[128,512]{1,0:T(8,128)(2,1)} custom-call(s32[2]{0:T(128)} %span_ref.1, bf16[128,512]{1,0:T(8,128)(2,1)} %qn_ref.1, bf16[128,256]{1,0:T(8,128)(2,1)} %qr_ref.1, bf16[128,576]{1,0:T(8,128)(2,1)} %copy.8.k_ref, bf16[512,512]{1,0:T(8,128)(2,1)} %ku_ref.1, bf16[512,512]{1,0:T(8,128)(2,1)} %vu_ref.1, bf16[512,2048]{1,0:T(8,128)(2,1)} %op_ref.1), custom_call_target="tpu_custom_call" | custom-call | tf_op jit(solution)/shard_map/attend/pallas_call | solution.py:363
  60.2 1.6 %copy.10 = bf16[128,512]{1,0:T(8,128)(2,1)} copy(bf16[128,512]{1,0:T(8,128)(2,1)} %attend.1) | data formatting | bytes 262144

commit v2 on v1

--- a/solution.py
+++ b/solution.py
@@ -16,8 +16,8 @@
 R = 4
 SUB = ROWS // R
 UNIT = HEADS_DEV * 4 * SUB
-KROWS = ROWS + 16
-HALVES = ((0, 64), (64, 80))
+KROWS = WIDTH + 16
+HALVES = ((0, 288), (288, 304))
 SCALE = (NOPE + ROPE) ** -0.5 * 1.4426950408889634
 LOG2E = 1.4426950408889634
 LOWEST = -1e30
@@ -56,26 +56,27 @@
     hm = ((h + 3) % 4, o, i)
 
     loads = [
-        pltpu.make_async_copy(k_ref, kbuf.at[0, pl.ds(0, ROWS)], load_sem.at[0]),
+        pltpu.make_async_copy(k_ref, kbuf.at[0, pl.ds(0, WIDTH)], load_sem.at[0]),
         pltpu.make_async_copy(qn_ref, qx.at[0, :, pl.ds(0, 512)], load_sem.at[1]),
         pltpu.make_async_copy(qr_ref, qx.at[0, :, pl.ds(512, 256)], load_sem.at[2]),
         pltpu.make_async_copy(ku_ref, ku, load_sem.at[3]),
         pltpu.make_async_copy(vu_ref, vu, load_sem.at[4]),
         pltpu.make_async_copy(op_ref, op, load_sem.at[5]),
     ]
+    barrier = pltpu.get_barrier_semaphore()
+    near = (sib, yp, ym, zp, zm, xs[1], xs[3])
+    for partner in near:
+        pl.semaphore_signal(barrier, inc=1, device_id=partner, device_id_type=MESH)
     for copy in loads:
         copy.start()
-    barrier = pltpu.get_barrier_semaphore()
-    for partner in (sib, yp, ym, zp, zm, xs[1], xs[2], xs[3], hp, hm):
-        pl.semaphore_signal(barrier, inc=1, device_id=partner, device_id_type=MESH)
     first = span_ref[0].astype(f32)
     second = span_ref[1].astype(f32)
     lane = lax.broadcasted_iota(jnp.int32, (16, 128), 1)
     row = lax.broadcasted_iota(jnp.int32, (16, 128), 0)
-    kbuf[0, ROWS:KROWS, :] = jnp.zeros((16, WIDTH), bf16)
-    kbuf[0, ROWS:KROWS, 0:128] = jnp.where(lane < SPAN, first, second).astype(bf16)
+    kbuf[0, WIDTH:KROWS, :] = jnp.where(lane < SPAN, first, second).astype(bf16)
     qpos[0] = jnp.where(row < 8, first, second).astype(bf16)
-    pl.semaphore_wait(barrier, 10)
+    loads[0].wait()
+    pl.semaphore_wait(barrier, len(near))
 
     sends = []
 
@@ -87,7 +88,7 @@
         copy.start()
         sends.append(copy)
 
-    count = [0]
+    count = [0, 0]
 
     def half(slot, b):
         begin, size = HALVES[b]
@@ -100,83 +101,81 @@
     def wait_k(slot, b):
         pltpu.make_async_copy(half(slot, b), half(slot, b), kr_sem.at[slot, b]).wait()
 
-    def qpart(slot, r):
-        return qx.at[slot, pl.ds(r * SUB, SUB)]
-
-    def send_q(slot, r, there, device, s_sem):
-        send(qpart(slot, r), qpart(there, r), s_sem, qr_sem.at[there, r], device)
-
-    def wait_q(slot, r):
-        pltpu.make_async_copy(qpart(slot, r), qpart(slot, r), qr_sem.at[slot, r]).wait()
-
-    loads[0].wait()
+    def qpart(slot, b):
+        return qx.at[slot, pl.ds(b * SPAN, SPAN)]
+
+    def send_q(slot, b, there, device):
+        send(qpart(slot, b), qpart(there, b), qs_sem.at[count[1]], qr_sem.at[there, b], device)
+        count[1] += 1
+
+    def wait_q(slot, b):
+        pltpu.make_async_copy(qpart(slot, b), qpart(slot, b), qr_sem.at[slot, b]).wait()
+
+    def send_pos(slot, there, device, n):
+        send(qpos.at[slot], qpos.at[there], ps_sem.at[n], pr_sem.at[there], device)
+
+    def wait_pos(slot):
+        pltpu.make_async_copy(qpos.at[slot], qpos.at[slot], pr_sem.at[slot]).wait()
+
     send_k(0, 0, 3, yp)
     send_k(0, 1, 1, ym)
     send_k(0, 0, 8, zp)
     send_k(0, 1, 8, zm)
     send_k(0, 0, 4, sib)
     send_k(0, 1, 4, sib)
+    send_pos(0, 3, xs[1], 0)
+    send_pos(0, 1, xs[3], 1)
+    loads[1].wait()
+    loads[2].wait()
+    send_q(0, 0, 3, xs[1])
+    send_q(0, 1, 1, xs[3])
     send_k(0, 1, 3, yp)
     send_k(0, 0, 1, ym)
-    loads[1].wait()
-    loads[2].wait()
-    for d in (1, 2, 3):
-        send(qpos.at[0], qpos.at[4 - d], ps_sem.at[d - 1], pr_sem.at[4 - d], xs[d])
-    for r in range(R):
-        send_q(0, r, 3, xs[1], qs_sem.at[0, r])
-        send_q(0, r, 1, xs[3], qs_sem.at[1, r])
-
-    def build_q(r):
-        rows = pl.ds(r * SUB, SUB)
+    send_q(0, 1, 3, xs[1])
+    send_q(0, 0, 1, xs[3])
+
+    within = lax.rem(lax.broadcasted_iota(jnp.int32, (ROWS, 128), 0), SPAN).astype(f32)
+
+    def build_q(d):
         for head in range(HEADS_DEV):
-            nope = qx[:, rows, head * NOPE : (head + 1) * NOPE].reshape(4 * SUB, NOPE)
             latent = lax.dot_general(
-                nope, ku[:, head * NOPE : (head + 1) * NOPE], TN, preferred_element_type=f32
+                qx[d, :, head * NOPE : (head + 1) * NOPE],
+                ku[:, head * NOPE : (head + 1) * NOPE], TN, preferred_element_type=f32,
             )
-            mine = pl.ds(head * 4 * SUB, 4 * SUB)
-            qs[r, mine, 0:LATENT] = latent.astype(bf16)
+            mine = slice(head * ROWS, (head + 1) * ROWS)
+            qs[d, mine, 0:LATENT] = latent.astype(bf16)
             begin = HEADS_DEV * NOPE + head * ROPE
-            qs[r, mine, LATENT:WIDTH] = qx[:, rows, begin : begin + ROPE].reshape(4 * SUB, ROPE)
-        within = lax.broadcasted_iota(jnp.int32, (SUB, 128), 0).astype(f32)
-        for d in range(4):
-            span = qpos[d].astype(f32)[(r * SUB // SPAN) * 8 : (r * SUB // SPAN) * 8 + 1, :]
-            pos = span * SPAN + (within + (r * SUB) % SPAN)
-            for head in range(HEADS_DEV):
-                qc[r, pl.ds(head * 4 * SUB + d * SUB, SUB), :] = pos
-        m_sc[r] = jnp.full((UNIT, 128), LOWEST, f32)
+            qs[d, mine, LATENT:WIDTH] = qx[d, :, begin : begin + ROPE]
+        spans = qpos[d].astype(f32)
+        span = jnp.concatenate(
+            [jnp.broadcast_to(spans[v : v + 1, :], (SPAN, 128)) for v in (0, 8)], axis=0
+        )
+        qc[d] = span * SPAN + within
 
     offset = lax.rem(lax.broadcasted_iota(jnp.int32, (1, 128), 1), SPAN).astype(f32)
-
-    def scores(chunk, r):
+    seen = set()
+
+    def scores(chunk, d):
         slots = CHUNKS[chunk]
-        keys = jnp.concatenate([kbuf[s, 0:ROWS, :] for s in slots], axis=0)
-        values = lax.dot_general(qs[r], keys, TN, preferred_element_type=f32)
-        rowpos = qc[r]
-        peak = m_sc[r]
-        for j, s in enumerate(slots):
-            keypos = kbuf[s, ROWS:KROWS, 0:128].astype(f32)[0:1, :] * SPAN + offset
-            part = jnp.where(
-                keypos <= rowpos, values[:, j * 128 : (j + 1) * 128] * SCALE, LOWEST
-            )
-            s_sc[r, :, s * 128 : (s + 1) * 128] = part
-            peak = jnp.maximum(peak, part)
-        m_sc[r] = peak
-
-    def scores_for(chunk, low, high):
-        def body(r, carry):
-            scores(chunk, r)
-            return carry
-
-        lax.fori_loop(low, high, body, 0)
-
-    def pass_z(slot):
-        send_k(slot, 0, slot + 8, zp)
-        send_k(slot, 1, slot + 8, zm)
-
-    wait_k(8, 0)
-    send_k(8, 0, 12, sib)
-    wait_k(8, 1)
-    send_k(8, 1, 12, sib)
+        keys = jnp.concatenate([kbuf[s, 0:WIDTH, :] for s in slots], axis=1)
+        values = lax.dot_general(qs[d], keys, NN, preferred_element_type=f32)
+        for head in range(HEADS_DEV):
+            rowpos = qc[d]
+            peak = m_sc[d, head] if d in seen else None
+            for j, s in enumerate(slots):
+                keypos = kbuf[s, WIDTH:KROWS, :].astype(f32)[0:1, :] * SPAN + offset
+                part = values[head * ROWS : (head + 1) * ROWS, j * 128 : (j + 1) * 128]
+                part = jnp.where(keypos <= rowpos, part * SCALE, LOWEST)
+                s_sc[d, head, :, s * 128 : (s + 1) * 128] = part
+                peak = part if peak is None else jnp.maximum(peak, part)
+            m_sc[d, head] = peak
+        seen.add(d)
+
+    loads[3].wait()
+    build_q(0)
+    for b in (0, 1):
+        wait_k(8, b)
+        send_k(8, b, 12, sib)
     wait_k(3, 0)
     send_k(3, 0, 2, yp)
     send_k(3, 0, 11, zp)
@@ -186,71 +185,66 @@
     send_k(1, 1, 9, zm)
     send_k(1, 1, 5, sib)
     wait_q(3, 0)
-    send_q(3, 0, 2, xs[1], qs_sem.at[2, 0])
+    send_q(3, 0, 2, xs[1])
+    wait_q(1, 1)
+    send_q(1, 1, 2, xs[3])
+    wait_pos(3)
+    send_pos(3, 2, xs[1], 2)
+    wait_pos(1)
+    for slot in (4, 12):
+        for b in (0, 1):
+            wait_k(slot, b)
+    scores(0, 0)
     wait_k(3, 1)
     send_k(3, 1, 11, zm)
     send_k(3, 1, 7, sib)
     wait_k(1, 0)
     send_k(1, 0, 9, zp)
     send_k(1, 0, 5, sib)
-    for d in (1, 2, 3):
-        pltpu.make_async_copy(qpos.at[d], qpos.at[d], pr_sem.at[d]).wait()
-    loads[3].wait()
+    wait_q(3, 1)
+    build_q(3)
     wait_q(1, 0)
-    wait_q(2, 0)
-    build_q(0)
-    for slot in (4, 12):
-        for b in (0, 1):
-            wait_k(slot, b)
-    scores(0, 0)
-    wait_q(1, 1)
-    send_q(1, 1, 2, xs[3], qs_sem.at[2, 1])
+    build_q(1)
     wait_k(2, 0)
     send_k(2, 0, 10, zp)
     send_k(2, 0, 6, sib)
     wait_k(2, 1)
     send_k(2, 1, 10, zm)
     send_k(2, 1, 6, sib)
-    wait_q(3, 1)
-    wait_q(2, 1)
-    build_q(1)
-    scores_for(0, 1, 2)
     for slot in (5, 7):
         for b in (0, 1):
             wait_k(slot, b)
-    wait_q(3, 2)
-    send_q(3, 2, 2, xs[1], qs_sem.at[2, 2])
-    scores_for(1, 0, 2)
-    for slot in (11, 9):
-        for b in (0, 1):
-            wait_k(slot, b)
-            send_k(slot, b, slot + 4, sib)
-    for b in (0, 1):
-        wait_k(6, b)
-    wait_q(1, 2)
-    wait_q(2, 2)
-    build_q(2)
-    scores_for(2, 0, 3)
+    scores(1, 0)
+    scores(0, 3)
+    scores(0, 1)
+    for slot, b in ((11, 0), (9, 1), (11, 1), (9, 0)):
+        wait_k(slot, b)
+        send_k(slot, b, slot + 4, sib)
+    scores(1, 3)
+    scores(1, 1)
     for b in (0, 1):
         wait_k(10, b)
         send_k(10, b, 14, sib)
-    wait_q(1, 3)
-    send_q(1, 3, 2, xs[3], qs_sem.at[2, 3])
-    scores_for(0, 2, 3)
-    scores_for(1, 2, 3)
-    for slot in (13, 14, 15):
+    for b in (0, 1):
+        wait_q(2, b)
+    wait_pos(2)
+    build_q(2)
+    scores(0, 2)
+    scores(1, 2)
+    for b in (0, 1):
+        wait_k(6, b)
+    for d in (0, 3, 1, 2):
+        scores(2, d)
+    for slot in (13, 15, 14):
         for b in (0, 1):
             wait_k(slot, b)
-    scores_for(3, 0, 3)
-    wait_q(3, 3)
-    wait_q(2, 3)
-    build_q(3)
-    for chunk in range(4):
-        scores_for(chunk, 3, 4)
+    for d in (0, 3, 1, 2):
+        scores(3, d)
     loads[4].wait()
 
     def weigh(r):
-        top = jnp.max(m_sc[r], axis=1, keepdims=True)
+        rows = slice(r * SUB, (r + 1) * SUB)
+        top = jnp.max(m_sc[:, :, rows, :].reshape(UNIT, 128), axis=1, keepdims=True)
         wide = jnp.broadcast_to(top, (UNIT, 128))
         total = jnp.zeros((UNIT, 128), f32)
         acc = None
@@ -258,28 +252,27 @@
             parts = []
             for j in range(4):
                 begin = (t * 4 + j) * 128
-                w = jnp.exp2(s_sc[r, :, begin : begin + 128] - wide)
+                w = jnp.exp2(s_sc[:, :, rows, begin : begin + 128].reshape(UNIT, 128) - wide)
                 total = total + w
                 parts.append(w.astype(bf16))
-            latents = jnp.concatenate([kbuf[t * 4 + j, 0:ROWS, 0:LATENT] for j in range(4)], axis=0)
+            latents = jnp.concatenate([kbuf[t * 4 + j, 0:LATENT, :] for j in range(4)], axis=1)
             piece = lax.dot_general(
-                jnp.concatenate(parts, axis=1), latents, NN, preferred_element_type=f32
+                jnp.concatenate(parts, axis=1), latents, TN, preferred_element_type=f32
             )
             acc = piece if acc is None else acc + piece
         denom = jnp.sum(total, axis=1, keepdims=True)
-        logs = top + jnp.log(denom) * LOG2E
-        latent_out = (acc / denom).astype(bf16)
+        logs = (top + jnp.log(denom) * LOG2E).reshape(4, HEADS_DEV, SUB, 1)
+        latent_out = (acc / denom).astype(bf16).reshape(4, HEADS_DEV, SUB, LATENT)
         for head in range(HEADS_DEV):
-            mine = slice(head * 4 * SUB, (head + 1) * 4 * SUB)
             part = lax.dot_general(
-                latent_out[mine], vu[:, head * 128 : (head + 1) * 128], NN,
-                preferred_element_type=f32,
+                latent_out[:, head].reshape(4 * SUB, LATENT),
+                vu[:, head * 128 : (head + 1) * 128], NN, preferred_element_type=f32,
             ).astype(bf16)
             for d in range(4):
                 pbuf[r, d, :, head * 128 : (head + 1) * 128] = part[d * SUB : (d + 1) * SUB]
-            flat = jnp.transpose(jnp.broadcast_to(logs[mine], (128, 128)))
+            flat = jnp.transpose(jnp.broadcast_to(logs[:, head].reshape(4 * SUB, 1), (128, 128)))
             stat[r, head : head + 1, :] = flat[0:1, :]
-        for d in (1, 3, 2):
+        for d in (2, 1, 3):
             send(pbuf.at[r, d], rbuf.at[r, d - 1], rs_sem.at[r, d - 1], rr_sem.at[r, d - 1], xs[d])
             send(stat.at[r], rstat.at[r, d - 1], ts_sem.at[r, d - 1], tr_sem.at[r, d - 1], xs[d])
 
@@ -367,16 +360,16 @@
         in_specs=[pl.BlockSpec(memory_space=pltpu.SMEM)] + [anywhere] * 6,
         out_specs=pl.BlockSpec(memory_space=pltpu.VMEM),
         scratch_shapes=[
-            pltpu.VMEM((16, KROWS, WIDTH), bf16),
+            pltpu.VMEM((16, KROWS, ROWS), bf16),
             pltpu.VMEM((4, ROWS, QWIDTH), bf16),
             pltpu.VMEM((4, 16, 128), bf16),
             pltpu.VMEM((512, 512), bf16),
             pltpu.VMEM((512, 512), bf16),
             pltpu.VMEM((512, 2048), bf16),
-            pltpu.VMEM((R, UNIT, WIDTH), bf16),
-            pltpu.VMEM((R, UNIT, 128), f32),
-            pltpu.VMEM((R, UNIT, 2048), f32),
-            pltpu.VMEM((R, UNIT, 128), f32),
+            pltpu.VMEM((4, HEADS_DEV * ROWS, WIDTH), bf16),
+            pltpu.VMEM((4, ROWS, 128), f32),
+            pltpu.VMEM((4, HEADS_DEV, ROWS, 16 * ROWS), f32),
+            pltpu.VMEM((4, HEADS_DEV, ROWS, 128), f32),
             pltpu.VMEM((R, 4, SUB, 512), bf16),
             pltpu.VMEM((R, 8, 128), f32),
             pltpu.VMEM((R, 3, SUB, 512), bf16),
@@ -388,8 +381,8 @@
             dma((6,)),
             dma((16, 2)),
             dma((40,)),
-            dma((4, R)),
-            dma((3, R)),
+            dma((4, 2)),
+            dma((6,)),
             dma((4,)),
             dma((3,)),
             dma((R, 3)),
@@ -402,7 +395,7 @@
         compiler_params=pltpu.CompilerParams(
             collective_id=0, has_side_effects=True, vmem_limit_bytes=62 * 2**20
         ),
-    )(span_ids, query_nope, query_rope, cache, key_up, value_up, out_proj)
+    )(span_ids, query_nope, query_rope, cache.T, key_up, value_up, out_proj)
 
 
 def solution(mesh):

time: 62.2 us -> 51.9 us (0.83)
  Pallas kernels: 58.5 us -> 50.2 us
  local copies, waits for them, and re-layouts: 3.27 us -> 1.57 us
    pallas_call x1, Pallas kernels: 58.5 us -> 50.2 us  [shards(): pl.pallas_call(kernel, name='attend', out_shape=jax.ShapeDtypeStruct((ROW...]
    unnamed x2 -> x1, local copies, waits for them, and re-layouts: 3.27 us -> 1.57 us
where the time goes in v2:
time: 51.9 us; the launch traced here: 51.8 us
  Pallas kernels  50.2 us (97%)
  local copies, waits for them, and re-layouts  1.57 us (3%)
    pallas_call x1, Pallas kernels, shards(): pl.pallas_call(kernel, name='attend', out_shape=jax.ShapeDtypeStruct((ROW...  50.2 us
    unnamed x1, local copies, waits for them, and re-layouts  1.57 us

profile of v2, /device:TPU:32, one launch (start us, length us, event | category | flops | bytes accessed | tf_op | source)
XLA Modules:
  0.0 51.8 jit_solution(15636304093736854899)
XLA Ops:
  0.0 50.2 %attend.1 = bf16[128,512]{1,0:T(8,128)(2,1)} custom-call(s32[2]{0:T(128)} %span_ref.1, bf16[128,512]{1,0:T(8,128)(2,1)} %qn_ref.1, bf16[128,256]{1,0:T(8,128)(2,1)} %qr_ref.1, bf16[576,128]{1,0:T(8,128)(2,1)} %bitcast.1, bf16[512,512]{1,0:T(8,128)(2,1)} %ku_ref.1, bf16[512,512]{1,0:T(8,128)(2,1)} %vu_ref.1, bf16[512,2048]{1,0:T(8,128)(2,1)} %op_ref.1), custom_call_target="tpu_custom_call" | custom-call | tf_op jit(solution)/shard_map/attend/pallas_call | solution.py:356
  50.2 1.6 %copy.9 = bf16[128,512]{1,0:T(8,128)(2,1)} copy(bf16[128,512]{1,0:T(8,128)(2,1)} %attend.1) | data formatting | bytes 262144

commit v3 on v2

--- a/solution.py
+++ b/solution.py
@@ -26,6 +26,14 @@
 NN = (((1,), (0,)), ((), ()))
 f32 = jnp.float32
 bf16 = jnp.bfloat16
+BOTH = (4, 5, 6, 7, 12, 13, 14, 15)
+KEY_SEM = {}
+for _slot in range(1, 16):
+    for _b in (0, 1):
+        if _slot in BOTH and _b == 1:
+            KEY_SEM[_slot, 1] = KEY_SEM[_slot, 0]
+        else:
+            KEY_SEM[_slot, _b] = len(set(KEY_SEM.values()))
 CHUNKS = ((0, 4, 8, 12), (1, 3, 5, 7), (2, 6, 9, 11), (10, 13, 14, 15))
 
 
@@ -33,8 +41,7 @@
     span_ref, qn_ref, qr_ref, k_ref, ku_ref, vu_ref, op_ref, out_ref,
     kbuf, qx, qpos, ku, vu, op, qs, qc, s_sc, m_sc, pbuf, stat, rbuf, rstat,
     ybuf, y1, ysum, y2,
-    load_sem, kr_sem, ks_sem, qr_sem, qs_sem, pr_sem, ps_sem, rr_sem, rs_sem, tr_sem, ts_sem,
-    zr_sem, zs_sem,
+    load_sem, kr_sem, qr_sem, pr_sem, rr_sem, tr_sem, zr_sem, send_sem,
 ):
     h = lax.axis_index("head")
     o = lax.axis_index("outer")
@@ -78,44 +85,42 @@
     loads[0].wait()
     pl.semaphore_wait(barrier, len(near))
 
-    sends = []
-
-    def send(src, dst, s_sem, r_sem, device):
-        copy = pltpu.make_async_remote_copy(
-            src_ref=src, dst_ref=dst, send_sem=s_sem, recv_sem=r_sem,
+    def send(src, dst, kind, r_sem, device):
+        pltpu.make_async_remote_copy(
+            src_ref=src, dst_ref=dst, send_sem=send_sem.at[kind], recv_sem=r_sem,
             device_id=device, device_id_type=MESH,
-        )
-        copy.start()
-        sends.append(copy)
-
-    count = [0, 0]
+        ).start()
+
+    def arrived(ref, sem):
+        pltpu.make_async_copy(ref, ref, sem).wait()
 
     def half(slot, b):
         begin, size = HALVES[b]
         return kbuf.at[slot, pl.ds(begin, size)]
 
     def send_k(slot, b, there, device):
-        send(half(slot, b), half(there, b), ks_sem.at[count[0]], kr_sem.at[there, b], device)
-        count[0] += 1
-
-    def wait_k(slot, b):
-        pltpu.make_async_copy(half(slot, b), half(slot, b), kr_sem.at[slot, b]).wait()
+        send(half(slot, b), half(there, b), 0, kr_sem.at[KEY_SEM[there, b]], device)
+
+    def wait_k(slot, b=None):
+        if slot in BOTH:
+            arrived(kbuf.at[slot], kr_sem.at[KEY_SEM[slot, 0]])
+        else:
+            arrived(half(slot, b), kr_sem.at[KEY_SEM[slot, b]])
 
     def qpart(slot, b):
         return qx.at[slot, pl.ds(b * SPAN, SPAN)]
 
     def send_q(slot, b, there, device):
-        send(qpart(slot, b), qpart(there, b), qs_sem.at[count[1]], qr_sem.at[there, b], device)
-        count[1] += 1
+        send(qpart(slot, b), qpart(there, b), 1, qr_sem.at[there - 1, b], device)
 
     def wait_q(slot, b):
-        pltpu.make_async_copy(qpart(slot, b), qpart(slot, b), qr_sem.at[slot, b]).wait()
-
-    def send_pos(slot, there, device, n):
-        send(qpos.at[slot], qpos.at[there], ps_sem.at[n], pr_sem.at[there], device)
+        arrived(qpart(slot, b), qr_sem.at[slot - 1, b])
+
+    def send_pos(slot, there, device):
+        send(qpos.at[slot], qpos.at[there], 2, pr_sem.at[there - 1], device)
 
     def wait_pos(slot):
-        pltpu.make_async_copy(qpos.at[slot], qpos.at[slot], pr_sem.at[slot]).wait()
+        arrived(qpos.at[slot], pr_sem.at[slot - 1])
 
     send_k(0, 0, 3, yp)
     send_k(0, 1, 1, ym)
@@ -123,8 +128,8 @@
     send_k(0, 1, 8, zm)
     send_k(0, 0, 4, sib)
     send_k(0, 1, 4, sib)
-    send_pos(0, 3, xs[1], 0)
-    send_pos(0, 1, xs[3], 1)
+    send_pos(0, 3, xs[1])
+    send_pos(0, 1, xs[3])
     loads[1].wait()
     loads[2].wait()
     send_q(0, 0, 3, xs[1])
@@ -155,27 +160,27 @@
     offset = lax.rem(lax.broadcasted_iota(jnp.int32, (1, 128), 1), SPAN).astype(f32)
     seen = set()
 
-    def scores(chunk, d):
+    def scores(chunk, sources):
         slots = CHUNKS[chunk]
         keys = jnp.concatenate([kbuf[s, 0:WIDTH, :] for s in slots], axis=1)
-        values = lax.dot_general(qs[d], keys, NN, preferred_element_type=f32)
-        for head in range(HEADS_DEV):
+        queries = jnp.concatenate([qs[d] for d in sources], axis=0)
+        values = lax.dot_general(queries, keys, NN, preferred_element_type=f32)
+        for n, d in enumerate(sources):
             rowpos = qc[d]
-            peak = m_sc[d, head] if d in seen else None
-            for j, s in enumerate(slots):
-                keypos = kbuf[s, WIDTH:KROWS, :].astype(f32)[0:1, :] * SPAN + offset
-                part = values[head * ROWS : (head + 1) * ROWS, j * 128 : (j + 1) * 128]
-                part = jnp.where(keypos <= rowpos, part * SCALE, LOWEST)
-                s_sc[d, head, :, s * 128 : (s + 1) * 128] = part
-                peak = part if peak is None else jnp.maximum(peak, part)
-            m_sc[d, head] = peak
-        seen.add(d)
+            for head in range(HEADS_DEV):
+                begin = (n * HEADS_DEV + head) * ROWS
+                peak = m_sc[d, head] if d in seen else None
+                for j, s in enumerate(slots):
+                    keypos = kbuf[s, WIDTH:KROWS, :].astype(f32)[0:1, :] * SPAN + offset
+                    part = values[begin : begin + ROWS, j * 128 : (j + 1) * 128]
+                    part = jnp.where(keypos <= rowpos, part * SCALE, LOWEST)
+                    s_sc[d, head, :, s * 128 : (s + 1) * 128] = part
+                    peak = part if peak is None else jnp.maximum(peak, part)
+                m_sc[d, head] = peak
+            seen.add(d)
 
     loads[3].wait()
     build_q(0)
-    for b in (0, 1):
-        wait_k(8, b)
-        send_k(8, b, 12, sib)
     wait_k(3, 0)
     send_k(3, 0, 2, yp)
     send_k(3, 0, 11, zp)
@@ -189,18 +194,20 @@
     wait_q(1, 1)
     send_q(1, 1, 2, xs[3])
     wait_pos(3)
-    send_pos(3, 2, xs[1], 2)
+    send_pos(3, 2, xs[1])
     wait_pos(1)
-    for slot in (4, 12):
-        for b in (0, 1):
-            wait_k(slot, b)
-    scores(0, 0)
+    for b in (0, 1):
+        wait_k(8, b)
+        send_k(8, b, 12, sib)
     wait_k(3, 1)
     send_k(3, 1, 11, zm)
     send_k(3, 1, 7, sib)
     wait_k(1, 0)
     send_k(1, 0, 9, zp)
     send_k(1, 0, 5, sib)
+    wait_k(4)
+    wait_k(12)
+    scores(0, (0,))
     wait_q(3, 1)
     build_q(3)
     wait_q(1, 0)
@@ -211,17 +218,14 @@
     wait_k(2, 1)
     send_k(2, 1, 10, zm)
     send_k(2, 1, 6, sib)
-    for slot in (5, 7):
-        for b in (0, 1):
-            wait_k(slot, b)
-    scores(1, 0)
-    scores(0, 3)
-    scores(0, 1)
+    scores(0, (3, 1))
     for slot, b in ((11, 0), (9, 1), (11, 1), (9, 0)):
         wait_k(slot, b)
         send_k(slot, b, slot + 4, sib)
-    scores(1, 3)
-    scores(1, 1)
+    wait_k(5)
+    wait_k(7)
+    scores(1, (0,))
+    scores(1, (3, 1))
     for b in (0, 1):
         wait_k(10, b)
         send_k(10, b, 14, sib)
@@ -229,22 +233,38 @@
         wait_q(2, b)
     wait_pos(2)
     build_q(2)
-    scores(0, 2)
-    scores(1, 2)
-    for b in (0, 1):
-        wait_k(6, b)
-    for d in (0, 3, 1, 2):
-        scores(2, d)
-    for slot in (13, 15, 14):
-        for b in (0, 1):
-            wait_k(slot, b)
-    for d in (0, 3, 1, 2):
-        scores(3, d)
+    scores(0, (2,))
+    scores(1, (2,))
+    wait_k(6)
+    scores(2, (0, 3))
+    scores(2, (1, 2))
+    wait_k(13)
+    wait_k(15)
+    wait_k(14)
     loads[4].wait()
 
     def weigh(r):
         rows = slice(r * SUB, (r + 1) * SUB)
-        top = jnp.max(m_sc[:, :, rows, :].reshape(UNIT, 128), axis=1, keepdims=True)
+        slots = CHUNKS[3]
+        pairs = [(d, head) for d in range(4) for head in range(HEADS_DEV)]
+        queries = jnp.concatenate(
+            [qs[d, head * ROWS + r * SUB : head * ROWS + (r + 1) * SUB, :] for d, head in pairs],
+            axis=0,
+        )
+        keys = jnp.concatenate([kbuf[s, 0:WIDTH, :] for s in slots], axis=1)
+        values = lax.dot_general(queries, keys, NN, preferred_element_type=f32)
+        peaks = []
+        for n, (d, head) in enumerate(pairs):
+            rowpos = qc[d, rows, :]
+            peak = m_sc[d, head, rows, :]
+            for j, s in enumerate(slots):
+                keypos = kbuf[s, WIDTH:KROWS, :].astype(f32)[0:1, :] * SPAN + offset
+                part = values[n * SUB : (n + 1) * SUB, j * 128 : (j + 1) * 128]
+                part = jnp.where(keypos <= rowpos, part * SCALE, LOWEST)
+                s_sc[d, head, rows, s * 128 : (s + 1) * 128] = part
+                peak = jnp.maximum(peak, part)
+            peaks.append(peak)
+        top = jnp.max(jnp.concatenate(peaks, axis=0), axis=1, keepdims=True)
         wide = jnp.broadcast_to(top, (UNIT, 128))
         total = jnp.zeros((UNIT, 128), f32)
         acc = None
@@ -262,24 +282,26 @@
             acc = piece if acc is None else acc + piece
         denom = jnp.sum(total, axis=1, keepdims=True)
         logs = (top + jnp.log(denom) * LOG2E).reshape(4, HEADS_DEV, SUB, 1)
-        latent_out = (acc / denom).astype(bf16).reshape(4, HEADS_DEV, SUB, LATENT)
-        for head in range(HEADS_DEV):
-            part = lax.dot_general(
+        latent_out = (acc * (1.0 / denom)).astype(bf16).reshape(4, HEADS_DEV, SUB, LATENT)
+        outs = [
+            lax.dot_general(
                 latent_out[:, head].reshape(4 * SUB, LATENT),
                 vu[:, head * 128 : (head + 1) * 128], NN, preferred_element_type=f32,
             ).astype(bf16)
+            for head in range(HEADS_DEV)
+        ]
+        for head in range(HEADS_DEV):
             for d in range(4):
-                pbuf[r, d, :, head * 128 : (head + 1) * 128] = part[d * SUB : (d + 1) * SUB]
+                pbuf[r, d, :, head * 128 : (head + 1) * 128] = outs[head][d * SUB : (d + 1) * SUB]
             flat = jnp.transpose(jnp.broadcast_to(logs[:, head].reshape(4 * SUB, 1), (128, 128)))
             stat[r, head : head + 1, :] = flat[0:1, :]
         for d in (2, 1, 3):
-            send(pbuf.at[r, d], rbuf.at[r, d - 1], rs_sem.at[r, d - 1], rr_sem.at[r, d - 1], xs[d])
-            send(stat.at[r], rstat.at[r, d - 1], ts_sem.at[r, d - 1], tr_sem.at[r, d - 1], xs[d])
+            send(pbuf.at[r, d], rbuf.at[r, d - 1], 3, rr_sem.at[r], xs[d])
+            send(stat.at[r], rstat.at[r, d - 1], 4, tr_sem.at[r], xs[d])
 
     def merge(r):
-        for d in (0, 1, 2):
-            pltpu.make_async_copy(rbuf.at[r, d], rbuf.at[r, d], rr_sem.at[r, d]).wait()
-            pltpu.make_async_copy(rstat.at[r, d], rstat.at[r, d], tr_sem.at[r, d]).wait()
+        arrived(rstat.at[r], tr_sem.at[r])
+        arrived(rbuf.at[r], rr_sem.at[r])
         tiles = [stat[r]] + [rstat[r, d] for d in range(3)]
         columns = [
             jnp.transpose(tile)[d * SUB : (d + 1) * SUB, :] for d, tile in enumerate(tiles)
@@ -303,29 +325,26 @@
             ).astype(bf16)
             if d == 2:
                 send(
-                    ybuf.at[r, 2, :, pl.ds(0, 256)], y1.at[r, 0],
-                    zs_sem.at[r, 0], zr_sem.at[r, 0], hp,
+                    ybuf.at[r, 2, :, pl.ds(0, 256)], y1.at[r, 0], 5, zr_sem.at[r, 0], hp,
                 )
                 send(
-                    ybuf.at[r, 2, :, pl.ds(256, 256)], y1.at[r, 1],
-                    zs_sem.at[r, 1], zr_sem.at[r, 1], hm,
+                    ybuf.at[r, 2, :, pl.ds(256, 256)], y1.at[r, 1], 5, zr_sem.at[r, 1], hm,
                 )
 
     def pass_on(r):
-        for b in (0, 1):
-            pltpu.make_async_copy(y1.at[r, b], y1.at[r, b], zr_sem.at[r, b]).wait()
+        arrived(y1.at[r, 0], zr_sem.at[r, 0])
         left = ybuf[r, 1, :, 0:256].astype(f32) + y1[r, 0].astype(f32)
         ysum[r, 0, :, 0:256] = left.astype(bf16)
         ysum[r, 0, :, 256:512] = ybuf[r, 1, :, 256:512]
-        send(ysum.at[r, 0], y2.at[r, 0], zs_sem.at[r, 2], zr_sem.at[r, 2], hp)
+        send(ysum.at[r, 0], y2.at[r, 0], 6, zr_sem.at[r, 2], hp)
+        arrived(y1.at[r, 1], zr_sem.at[r, 1])
         right = ybuf[r, 3, :, 256:512].astype(f32) + y1[r, 1].astype(f32)
         ysum[r, 1, :, 256:512] = right.astype(bf16)
         ysum[r, 1, :, 0:256] = ybuf[r, 3, :, 0:256]
-        send(ysum.at[r, 1], y2.at[r, 1], zs_sem.at[r, 3], zr_sem.at[r, 3], hm)
+        send(ysum.at[r, 1], y2.at[r, 1], 6, zr_sem.at[r, 2], hm)
 
     def finish(r):
-        for b in (0, 1):
-            pltpu.make_async_copy(y2.at[r, b], y2.at[r, b], zr_sem.at[r, 2 + b]).wait()
+        arrived(y2.at[r], zr_sem.at[r, 2])
         total = ybuf[r, 0].astype(f32) + y2[r, 0].astype(f32) + y2[r, 1].astype(f32)
         out_ref[r * SUB : (r + 1) * SUB, :] = total.astype(bf16)
 
@@ -346,8 +365,10 @@
     finish(1)
     finish(2)
     finish(3)
-    for copy in sends:
-        copy.wait_send()
+    for kind, ref in enumerate((
+        kbuf.at[pl.ds(0, 15)], qx.at[pl.ds(0, 3)], qpos.at[pl.ds(0, 3)], rbuf, rstat, y1, y2,
+    )):
+        arrived(ref, send_sem.at[kind])
 
 
 def shards(query_nope, query_rope, cache, span_ids, key_up, value_up, out_proj):
@@ -379,23 +400,21 @@
             pltpu.VMEM((R, 2, SUB, 512), bf16),
             pltpu.VMEM((R, 2, SUB, 512), bf16),
             dma((6,)),
-            dma((16, 2)),
-            dma((40,)),
-            dma((4, 2)),
-            dma((6,)),
-            dma((4,)),
+            dma((len(set(KEY_SEM.values())),)),
+            dma((3, 2)),
             dma((3,)),
+            dma((R,)),
+            dma((R,)),
             dma((R, 3)),
-            dma((R, 3)),
-            dma((R, 3)),
-            dma((R, 3)),
-            dma((R, 4)),
-            dma((R, 4)),
+            dma((7,)),
         ],
         compiler_params=pltpu.CompilerParams(
-            collective_id=0, has_side_effects=True, vmem_limit_bytes=62 * 2**20
+            collective_id=0, has_side_effects=True, vmem_limit_bytes=48 * 2**20
         ),
-    )(span_ids, query_nope, query_rope, cache.T, key_up, value_up, out_proj)
+    )(*(
+        pltpu.with_memory_space_constraint(a, pltpu.HBM)
+        for a in (span_ids, query_nope, query_rope, cache.T, key_up, value_up, out_proj)
+    ))
 
 
 def solution(mesh):

time: 51.9 us -> 48.3 us (0.931)
  Pallas kernels: 50.2 us -> 47.6 us
  local copies, waits for them, and re-layouts: 1.57 us -> 0.66 us
    pallas_call x1, Pallas kernels: 50.2 us -> 47.6 us  [shards(): pl.pallas_call(kernel, name='attend', out_shape=jax.ShapeDtypeStruct((ROW...]
    unnamed x1, local copies, waits for them, and re-layouts: 1.57 us -> 0.66 us
where the time goes in v3:
time: 48.3 us; the launch traced here: 48.2 us
  Pallas kernels  47.6 us (99%)
  local copies, waits for them, and re-layouts  0.66 us (1%)
    pallas_call x1, Pallas kernels, shards(): pl.pallas_call(kernel, name='attend', out_shape=jax.ShapeDtypeStruct((ROW...  47.6 us

profile of v3, /device:TPU:32, one launch (start us, length us, event | category | flops | bytes accessed | tf_op | source)
XLA Modules:
  0.0 48.2 jit_solution(3641084149407992044)
XLA Ops:
  0.0 47.6 %attend.1 = bf16[128,512]{1,0:T(8,128)(2,1)S(1)} custom-call(s32[2]{0:T(128)} %span_ref.1, bf16[128,512]{1,0:T(8,128)(2,1)} %qn_ref.1, bf16[128,256]{1,0:T(8,128)(2,1)} %qr_ref.1, bf16[576,128]{1,0:T(8,128)(2,1)} %bitcast.1, bf16[512,512]{1,0:T(8,128)(2,1)} %ku_ref.1, bf16[512,512]{1,0:T(8,128)(2,1)} %vu_ref.1, bf16[512,2048]{1,0:T(8,128)(2,1)} %op_ref.1), custom_call_target="tpu_custom_call" | custom-call | tf_op jit(solution)/shard_map/attend/pallas_call | solution.py:377
  47.6 0.7 %copy.9 = bf16[128,512]{1,0:T(8,128)(2,1)} copy(bf16[128,512]{1,0:T(8,128)(2,1)S(1)} %attend.1) | data formatting | bytes 262144

commit v4 on v3

--- a/solution.py
+++ b/solution.py
@@ -12,34 +12,33 @@
 HEADS_DEV = 4
 ROWS = 128
 WIDTH = LATENT + ROPE
+QK = NOPE + ROPE
 QWIDTH = HEADS_DEV * (NOPE + ROPE)
 R = 4
 SUB = ROWS // R
-UNIT = HEADS_DEV * 4 * SUB
 KROWS = WIDTH + 16
-HALVES = ((0, 288), (288, 304))
+PIECES = ((0, 144), (144, 144), (288, 144), (432, 160))
 SCALE = (NOPE + ROPE) ** -0.5 * 1.4426950408889634
 LOG2E = 1.4426950408889634
 LOWEST = -1e30
 MESH = pl.DeviceIdType.MESH
-TN = (((1,), (1,)), ((), ()))
 NN = (((1,), (0,)), ((), ()))
 f32 = jnp.float32
 bf16 = jnp.bfloat16
 BOTH = (4, 5, 6, 7, 12, 13, 14, 15)
 KEY_SEM = {}
 for _slot in range(1, 16):
-    for _b in (0, 1):
-        if _slot in BOTH and _b == 1:
-            KEY_SEM[_slot, 1] = KEY_SEM[_slot, 0]
+    for _p in range(4):
+        if _slot in BOTH and _p:
+            KEY_SEM[_slot, _p] = KEY_SEM[_slot, 0]
         else:
-            KEY_SEM[_slot, _b] = len(set(KEY_SEM.values()))
+            KEY_SEM[_slot, _p] = len(set(KEY_SEM.values()))
 CHUNKS = ((0, 4, 8, 12), (1, 3, 5, 7), (2, 6, 9, 11), (10, 13, 14, 15))
 
 
 def kernel(
     span_ref, qn_ref, qr_ref, k_ref, ku_ref, vu_ref, op_ref, out_ref,
-    kbuf, qx, qpos, ku, vu, op, qs, qc, s_sc, m_sc, pbuf, stat, rbuf, rstat,
+    kbuf, qx, qpos, ku, vu, op, wk, kt, v_sc, qs, qc, s_sc, m_sc, pbuf, stat, rbuf, rstat,
     ybuf, y1, ysum, y2,
     load_sem, kr_sem, qr_sem, pr_sem, rr_sem, tr_sem, zr_sem, send_sem,
 ):
@@ -94,18 +93,21 @@
     def arrived(ref, sem):
         pltpu.make_async_copy(ref, ref, sem).wait()
 
-    def half(slot, b):
-        begin, size = HALVES[b]
+    def piece(slot, p):
+        begin, size = PIECES[p]
         return kbuf.at[slot, pl.ds(begin, size)]
 
-    def send_k(slot, b, there, device):
-        send(half(slot, b), half(there, b), 0, kr_sem.at[KEY_SEM[there, b]], device)
-
-    def wait_k(slot, b=None):
-        if slot in BOTH:
+    def send_k(slot, p, there, device):
+        send(piece(slot, p), piece(there, p), 0, kr_sem.at[KEY_SEM[there, p]], device)
+
+    def to_sib(slot):
+        send(kbuf.at[slot], kbuf.at[slot + 4], 0, kr_sem.at[KEY_SEM[slot + 4, 0]], sib)
+
+    def wait_k(slot, p=None):
+        if p is None:
             arrived(kbuf.at[slot], kr_sem.at[KEY_SEM[slot, 0]])
         else:
-            arrived(half(slot, b), kr_sem.at[KEY_SEM[slot, b]])
+            arrived(piece(slot, p), kr_sem.at[KEY_SEM[slot, p]])
 
     def qpart(slot, b):
         return qx.at[slot, pl.ds(b * SPAN, SPAN)]
@@ -122,20 +124,21 @@
     def wait_pos(slot):
         arrived(qpos.at[slot], pr_sem.at[slot - 1])
 
-    send_k(0, 0, 3, yp)
-    send_k(0, 1, 1, ym)
-    send_k(0, 0, 8, zp)
-    send_k(0, 1, 8, zm)
-    send_k(0, 0, 4, sib)
-    send_k(0, 1, 4, sib)
+    for p in (0, 1):
+        send_k(0, p, 3, yp)
+        send_k(0, p + 2, 1, ym)
+        send_k(0, p, 8, zp)
+        send_k(0, p + 2, 8, zm)
+    to_sib(0)
     send_pos(0, 3, xs[1])
     send_pos(0, 1, xs[3])
     loads[1].wait()
     loads[2].wait()
     send_q(0, 0, 3, xs[1])
     send_q(0, 1, 1, xs[3])
-    send_k(0, 1, 3, yp)
-    send_k(0, 0, 1, ym)
+    for p in (0, 1):
+        send_k(0, p + 2, 3, yp)
+        send_k(0, p, 1, ym)
     send_q(0, 1, 3, xs[1])
     send_q(0, 0, 1, xs[3])
 
@@ -143,14 +146,10 @@
 
     def build_q(d):
         for head in range(HEADS_DEV):
-            latent = lax.dot_general(
-                qx[d, :, head * NOPE : (head + 1) * NOPE],
-                ku[:, head * NOPE : (head + 1) * NOPE], TN, preferred_element_type=f32,
-            )
-            mine = slice(head * ROWS, (head + 1) * ROWS)
-            qs[d, mine, 0:LATENT] = latent.astype(bf16)
+            mine = slice(d * ROWS, (d + 1) * ROWS)
+            qs[head, mine, 0:NOPE] = qx[d, :, head * NOPE : (head + 1) * NOPE]
             begin = HEADS_DEV * NOPE + head * ROPE
-            qs[d, mine, LATENT:WIDTH] = qx[d, :, begin : begin + ROPE]
+            qs[head, mine, NOPE:QK] = qx[d, :, begin : begin + ROPE]
         spans = qpos[d].astype(f32)
         span = jnp.concatenate(
             [jnp.broadcast_to(spans[v : v + 1, :], (SPAN, 128)) for v in (0, 8)], axis=0
@@ -158,37 +157,54 @@
         qc[d] = span * SPAN + within
 
     offset = lax.rem(lax.broadcasted_iota(jnp.int32, (1, 128), 1), SPAN).astype(f32)
-    seen = set()
+
+    def lift(chunk):
+        slots = CHUNKS[chunk]
+        where = slice(chunk * 512, (chunk + 1) * 512)
+        latents = jnp.concatenate([kbuf[s, 0:LATENT, :] for s in slots], axis=1)
+        keys = lax.dot_general(wk[...], latents, NN, preferred_element_type=f32).astype(bf16)
+        ropes = jnp.concatenate([kbuf[s, LATENT:WIDTH, :] for s in slots], axis=1)
+        for head in range(HEADS_DEV):
+            kt[head, 0:NOPE, where] = keys[head * NOPE : (head + 1) * NOPE]
+            kt[head, NOPE:QK, where] = ropes
+        v_sc[where, :] = lax.dot_general(
+            latents, vu[...], (((0,), (0,)), ((), ())), preferred_element_type=f32
+        ).astype(bf16)
+
+    def masked(values, slot, rowpos):
+        keypos = kbuf[slot, WIDTH:KROWS, :].astype(f32)[0:1, :] * SPAN + offset
+        return jnp.where(keypos <= rowpos, values * SCALE, LOWEST)
 
     def scores(chunk, sources):
-        slots = CHUNKS[chunk]
-        keys = jnp.concatenate([kbuf[s, 0:WIDTH, :] for s in slots], axis=1)
-        queries = jnp.concatenate([qs[d] for d in sources], axis=0)
-        values = lax.dot_general(queries, keys, NN, preferred_element_type=f32)
-        for n, d in enumerate(sources):
-            rowpos = qc[d]
-            for head in range(HEADS_DEV):
-                begin = (n * HEADS_DEV + head) * ROWS
-                peak = m_sc[d, head] if d in seen else None
-                for j, s in enumerate(slots):
-                    keypos = kbuf[s, WIDTH:KROWS, :].astype(f32)[0:1, :] * SPAN + offset
-                    part = values[begin : begin + ROWS, j * 128 : (j + 1) * 128]
-                    part = jnp.where(keypos <= rowpos, part * SCALE, LOWEST)
-                    s_sc[d, head, :, s * 128 : (s + 1) * 128] = part
+        for head in range(HEADS_DEV):
+            queries = jnp.concatenate(
+                [qs[head, d * ROWS : (d + 1) * ROWS, :] for d in sources], axis=0
+            )
+            values = lax.dot_general(
+                queries, kt[head, :, chunk * 512 : (chunk + 1) * 512], NN,
+                preferred_element_type=f32,
+            )
+            for n, d in enumerate(sources):
+                rowpos = qc[d]
+                peak = m_sc[d, head] if chunk else None
+                for j, slot in enumerate(CHUNKS[chunk]):
+                    part = values[n * ROWS : (n + 1) * ROWS, j * 128 : (j + 1) * 128]
+                    part = masked(part, slot, rowpos)
+                    begin = chunk * 512 + j * 128
+                    s_sc[d, head, :, begin : begin + 128] = part
                     peak = part if peak is None else jnp.maximum(peak, part)
                 m_sc[d, head] = peak
-            seen.add(d)
-
+
+    build_q(0)
     loads[3].wait()
-    build_q(0)
-    wait_k(3, 0)
-    send_k(3, 0, 2, yp)
-    send_k(3, 0, 11, zp)
-    send_k(3, 0, 7, sib)
-    wait_k(1, 1)
-    send_k(1, 1, 2, ym)
-    send_k(1, 1, 9, zm)
-    send_k(1, 1, 5, sib)
+    wk[...] = jnp.transpose(ku[...])
+    for p in (0, 1):
+        wait_k(3, p)
+        send_k(3, p, 2, yp)
+        send_k(3, p, 11, zp)
+        wait_k(1, p + 2)
+        send_k(1, p + 2, 2, ym)
+        send_k(1, p + 2, 9, zm)
     wait_q(3, 0)
     send_q(3, 0, 2, xs[1])
     wait_q(1, 1)
@@ -196,104 +212,99 @@
     wait_pos(3)
     send_pos(3, 2, xs[1])
     wait_pos(1)
-    for b in (0, 1):
-        wait_k(8, b)
-        send_k(8, b, 12, sib)
-    wait_k(3, 1)
-    send_k(3, 1, 11, zm)
-    send_k(3, 1, 7, sib)
-    wait_k(1, 0)
-    send_k(1, 0, 9, zp)
-    send_k(1, 0, 5, sib)
+    for p in range(4):
+        wait_k(8, p)
+    to_sib(8)
+    for p in (0, 1):
+        wait_k(3, p + 2)
+        send_k(3, p + 2, 11, zm)
+        wait_k(1, p)
+        send_k(1, p, 9, zp)
+    to_sib(3)
+    to_sib(1)
+    loads[4].wait()
     wait_k(4)
     wait_k(12)
+    lift(0)
+    for p in (0, 1):
+        wait_k(2, p)
+        send_k(2, p, 10, zp)
+        wait_k(2, p + 2)
+        send_k(2, p + 2, 10, zm)
+    to_sib(2)
     scores(0, (0,))
     wait_q(3, 1)
     build_q(3)
     wait_q(1, 0)
     build_q(1)
-    wait_k(2, 0)
-    send_k(2, 0, 10, zp)
-    send_k(2, 0, 6, sib)
-    wait_k(2, 1)
-    send_k(2, 1, 10, zm)
-    send_k(2, 1, 6, sib)
     scores(0, (3, 1))
-    for slot, b in ((11, 0), (9, 1), (11, 1), (9, 0)):
-        wait_k(slot, b)
-        send_k(slot, b, slot + 4, sib)
     wait_k(5)
     wait_k(7)
-    scores(1, (0,))
-    scores(1, (3, 1))
-    for b in (0, 1):
-        wait_k(10, b)
-        send_k(10, b, 14, sib)
+    lift(1)
+    scores(1, (0, 3, 1))
+    for slot in (11, 9):
+        for p in range(4):
+            wait_k(slot, p)
+        to_sib(slot)
     for b in (0, 1):
         wait_q(2, b)
     wait_pos(2)
     build_q(2)
     scores(0, (2,))
+    for p in range(4):
+        wait_k(10, p)
+    to_sib(10)
     scores(1, (2,))
     wait_k(6)
-    scores(2, (0, 3))
-    scores(2, (1, 2))
+    lift(2)
+    scores(2, (0, 1, 2, 3))
     wait_k(13)
     wait_k(15)
     wait_k(14)
-    loads[4].wait()
+    lift(3)
 
     def weigh(r):
         rows = slice(r * SUB, (r + 1) * SUB)
-        slots = CHUNKS[3]
-        pairs = [(d, head) for d in range(4) for head in range(HEADS_DEV)]
-        queries = jnp.concatenate(
-            [qs[d, head * ROWS + r * SUB : head * ROWS + (r + 1) * SUB, :] for d, head in pairs],
-            axis=0,
-        )
-        keys = jnp.concatenate([kbuf[s, 0:WIDTH, :] for s in slots], axis=1)
-        values = lax.dot_general(queries, keys, NN, preferred_element_type=f32)
-        peaks = []
-        for n, (d, head) in enumerate(pairs):
-            rowpos = qc[d, rows, :]
-            peak = m_sc[d, head, rows, :]
-            for j, s in enumerate(slots):
-                keypos = kbuf[s, WIDTH:KROWS, :].astype(f32)[0:1, :] * SPAN + offset
-                part = values[n * SUB : (n + 1) * SUB, j * 128 : (j + 1) * 128]
-                part = jnp.where(keypos <= rowpos, part * SCALE, LOWEST)
-                s_sc[d, head, rows, s * 128 : (s + 1) * 128] = part
+        heads = range(HEADS_DEV)
+        rowpos = qc[:, rows, :].reshape(4 * SUB, 128)
+        scored, tops = [], []
+        for head in heads:
+            queries = jnp.concatenate(
+                [qs[head, d * ROWS + r * SUB : d * ROWS + (r + 1) * SUB, :] for d in range(4)],
+                axis=0,
+            )
+            scored.append(
+                lax.dot_general(queries, kt[head, :, 1536:2048], NN, preferred_element_type=f32)
+            )
+        for head in heads:
+            peak = m_sc[:, head, rows, :].reshape(4 * SUB, 128)
+            for j, slot in enumerate(CHUNKS[3]):
+                part = masked(scored[head][:, j * 128 : (j + 1) * 128], slot, rowpos)
+                s_sc[:, head, rows, 1536 + j * 128 : 1664 + j * 128] = part.reshape(4, SUB, 128)
                 peak = jnp.maximum(peak, part)
-            peaks.append(peak)
-        top = jnp.max(jnp.concatenate(peaks, axis=0), axis=1, keepdims=True)
-        wide = jnp.broadcast_to(top, (UNIT, 128))
-        total = jnp.zeros((UNIT, 128), f32)
-        acc = None
-        for t in range(4):
+            tops.append(jnp.max(peak, axis=1, keepdims=True))
+        totals, accs = [], []
+        for head in heads:
+            wide = jnp.broadcast_to(tops[head], (4 * SUB, 128))
+            total = None
             parts = []
-            for j in range(4):
-                begin = (t * 4 + j) * 128
-                w = jnp.exp2(s_sc[:, :, rows, begin : begin + 128].reshape(UNIT, 128) - wide)
-                total = total + w
+            for n in range(16):
+                value = s_sc[:, head, rows, n * 128 : (n + 1) * 128].reshape(4 * SUB, 128)
+                w = jnp.exp2(value - wide)
+                total = w if total is None else total + w
                 parts.append(w.astype(bf16))
-            latents = jnp.concatenate([kbuf[t * 4 + j, 0:LATENT, :] for j in range(4)], axis=1)
-            piece = lax.dot_general(
-                jnp.concatenate(parts, axis=1), latents, TN, preferred_element_type=f32
-            )
-            acc = piece if acc is None else acc + piece
-        denom = jnp.sum(total, axis=1, keepdims=True)
-        logs = (top + jnp.log(denom) * LOG2E).reshape(4, HEADS_DEV, SUB, 1)
-        latent_out = (acc * (1.0 / denom)).astype(bf16).reshape(4, HEADS_DEV, SUB, LATENT)
-        outs = [
-            lax.dot_general(
-                latent_out[:, head].reshape(4 * SUB, LATENT),
-                vu[:, head * 128 : (head + 1) * 128], NN, preferred_element_type=f32,
-            ).astype(bf16)
-            for head in range(HEADS_DEV)
-        ]
+            totals.append(total)
+            accs.append(lax.dot_general(
+                jnp.concatenate(parts, axis=1), v_sc[:, head * 128 : (head + 1) * 128], NN,
+                preferred_element_type=f32,
+            ))
+        denoms = [jnp.sum(total, axis=1, keepdims=True) for total in totals]
+        logs = [top + jnp.log(denom) * LOG2E for top, denom in zip(tops, denoms)]
+        outs = [(acc * (1.0 / denom)).astype(bf16) for acc, denom in zip(accs, denoms)]
         for head in range(HEADS_DEV):
             for d in range(4):
                 pbuf[r, d, :, head * 128 : (head + 1) * 128] = outs[head][d * SUB : (d + 1) * SUB]
-            flat = jnp.transpose(jnp.broadcast_to(logs[:, head].reshape(4 * SUB, 1), (128, 128)))
+            flat = jnp.transpose(jnp.broadcast_to(logs[head], (128, 128)))
             stat[r, head : head + 1, :] = flat[0:1, :]
         for d in (2, 1, 3):
             send(pbuf.at[r, d], rbuf.at[r, d - 1], 3, rr_sem.at[r], xs[d])
@@ -348,23 +359,15 @@
         total = ybuf[r, 0].astype(f32) + y2[r, 0].astype(f32) + y2[r, 1].astype(f32)
         out_ref[r * SUB : (r + 1) * SUB, :] = total.astype(bf16)
 
-    weigh(0)
-    weigh(1)
-    weigh(2)
+    for r in range(R):
+        weigh(r)
     loads[5].wait()
-    merge(0)
-    weigh(3)
-    merge(1)
-    pass_on(0)
-    merge(2)
-    pass_on(1)
-    merge(3)
-    pass_on(2)
-    finish(0)
-    pass_on(3)
-    finish(1)
-    finish(2)
-    finish(3)
+    for r in range(R):
+        merge(r)
+    for r in range(R):
+        pass_on(r)
+    for r in range(R):
+        finish(r)
     for kind, ref in enumerate((
         kbuf.at[pl.ds(0, 15)], qx.at[pl.ds(0, 3)], qpos.at[pl.ds(0, 3)], rbuf, rstat, y1, y2,
     )):
@@ -387,7 +390,10 @@
             pltpu.VMEM((512, 512), bf16),
             pltpu.VMEM((512, 512), bf16),
             pltpu.VMEM((512, 2048), bf16),
-            pltpu.VMEM((4, HEADS_DEV * ROWS, WIDTH), bf16),
+            pltpu.VMEM((512, LATENT), bf16),
+            pltpu.VMEM((HEADS_DEV, QK, 16 * ROWS), bf16),
+            pltpu.VMEM((16 * ROWS, 512), bf16),
+            pltpu.VMEM((HEADS_DEV, 4 * ROWS, QK), bf16),
             pltpu.VMEM((4, ROWS, 128), f32),
             pltpu.VMEM((4, HEADS_DEV, ROWS, 16 * ROWS), f32),
             pltpu.VMEM((4, HEADS_DEV, ROWS, 128), f32),

time: 48.3 us -> 42.9 us (0.89); the launches traced: 48.2 us -> 42.3 us
  Pallas kernels: 47.6 us -> 41.7 us
    pallas_call x1, Pallas kernels: 47.6 us -> 41.7 us  [shards(): pl.pallas_call(kernel, name='attend', out_shape=jax.ShapeDtypeStruct((ROW...]
where the time goes in v4:
time: 42.9 us; the launch traced here: 42.3 us
  Pallas kernels  41.7 us (97%)
  local copies, waits for them, and re-layouts  0.66 us (2%)
    pallas_call x1, Pallas kernels, shards(): pl.pallas_call(kernel, name='attend', out_shape=jax.ShapeDtypeStruct((ROW...  41.7 us

profile of v4, /device:TPU:32, one launch (start us, length us, event | category | flops | bytes accessed | tf_op | source)
XLA Modules:
  0.0 42.3 jit_solution(8611564708754361017)
XLA Ops:
  0.0 41.7 %attend.1 = bf16[128,512]{1,0:T(8,128)(2,1)S(1)} custom-call(s32[2]{0:T(128)} %span_ref.1, bf16[128,512]{1,0:T(8,128)(2,1)} %qn_ref.1, bf16[128,256]{1,0:T(8,128)(2,1)} %qr_ref.1, bf16[576,128]{1,0:T(8,128)(2,1)} %bitcast.1, bf16[512,512]{1,0:T(8,128)(2,1)} %ku_ref.1, bf16[512,512]{1,0:T(8,128)(2,1)} %vu_ref.1, bf16[512,2048]{1,0:T(8,128)(2,1)} %op_ref.1), custom_call_target="tpu_custom_call" | custom-call | tf_op jit(solution)/shard_map/attend/pallas_call | solution.py:380
  41.7 0.7 %copy.9 = bf16[128,512]{1,0:T(8,128)(2,1)} copy(bf16[128,512]{1,0:T(8,128)(2,1)S(1)} %attend.1) | data formatting | bytes 262144
